TPU v7x, 512 devices: a whole 4x4x16 slice. The times are simulated.
512 devices in a mesh: dp: 128 (over y, z, core), mp: 4 (over x).
Axes of the slice: x: 4, y: 4, z: 16, core: 2. Of those that a mesh axis runs over, the one named last changes fastest.
Arguments:
- hidden: bfloat16 [90112, 7168], P('dp', 'mp'), may hold values from -0.1875 to 0.1875
- router_weight: bfloat16 [7168, 256], P(('mp', 'dp')), may hold values from -3 to 3
- logits: float32 [90112, 256], P(('dp', 'mp')), may hold values from -12 to 240
- first_pot: float32 [256], replicated, may hold values from -1 to 1
- second_pot: float32 [256], replicated, may hold values from -1 to 1
- expert_index: int32 [90112], P(('dp', 'mp')), may hold values from 0 to 255
- loss_grad: float32 [90112], P(('dp', 'mp')), may hold values from -9 to 9
Outputs:
- weight_grad: float32 [7168, 256], P(('mp', 'dp'))
- hidden_grad: bfloat16 [90112, 7168], P('dp', 'mp')
All inputs are finite; a program needn't handle non-finite values.
Results may differ from a plain program's by a relative error of at most 0.005.
Values may be sent and summed in bfloat16 or wider, within the bound.
No kernel may reach another device: no remote copies, remote signals or barrier semaphores. Data moves between devices by JAX's collectives and lax.ppermute only.
A program may use at most 64 MiB of HBM per device.

v0:
```python
import jax
import jax.numpy as jnp
from jax import lax
from jax.sharding import Mesh
from jax.sharding import PartitionSpec as P

DP = ("dp_0", "dp_1", "dp_2")
DP_MP = ("dp_0", "dp_1", "dp_2", "mp")
MP_DP = ("mp", "dp_0", "dp_1", "dp_2")


def copy_for_each(array, axis):
    devices = lax.axis_size(axis)
    return lax.all_to_all(
        jnp.broadcast_to(array[None], (devices, *array.shape)), axis, 0, 0, tiled=True
    )


def over_copies(array, axis):
    everything = copy_for_each(array, axis)
    return jnp.sum(everything, axis=0)


def by_axis(array, axes):
    far, near = axes
    nearer = over_copies(array, near)
    return over_copies(nearer, far)


def laid_out(pieces, dim):
    lengths = list(pieces.shape[1:])
    lengths[dim] *= pieces.shape[0]
    return jnp.moveaxis(pieces, 0, dim).reshape(lengths)


def collect(array, axis, dim):
    return laid_out(copy_for_each(array, axis), dim)


def whole_of(array, axes, dim):
    far, near = axes
    leading = copy_for_each(array, far)
    pieces = jnp.swapaxes(copy_for_each(leading, near), 0, 1)
    return laid_out(pieces.reshape(-1, *array.shape), dim)


def cut_along(array, dim, devices):
    before, after = (array.shape[:dim], array.shape[dim + 1 :])
    return jnp.moveaxis(array.reshape(*before, devices, -1, *after), dim, 0)


def sum_at_owner(array, axis, dim):
    devices = lax.axis_size(axis)
    pieces = lax.all_to_all(cut_along(array, dim, devices), axis, 0, 0, tiled=True)
    return jnp.sum(pieces, axis=0)


def summed_rows(array, axes, dim):
    far, near = axes
    pieces = cut_along(array, dim, lax.axis_size(far))
    nearer = sum_at_owner(pieces, near, dim + 1)
    arrived = lax.all_to_all(nearer, far, split_axis=0, concat_axis=0, tiled=True)
    return arrived.sum(axis=0)


def neg_lse(values):
    top = jnp.max(values, axis=1, keepdims=True)
    return -(top[:, 0] + jnp.log(jnp.sum(jnp.exp(values - top), axis=1)))


def body(hidden, router_weight, logits, first_pot, second_pot, expert_index, loss_grad):
    experts = logits.shape[1]
    total_tokens = logits.shape[0] * lax.axis_size(DP) * lax.axis_size("mp")
    ratio = experts / total_tokens
    first_row = neg_lse(logits)
    first_soft = jnp.exp(logits + first_row[:, None])
    shifted = logits + first_pot[None, :]
    second_row = neg_lse(shifted)
    second_soft = jnp.exp(shifted + second_row[:, None])
    first_col = ratio * jnp.exp(logits + first_row[:, None] + first_pot[None, :])
    prob = jnp.exp(logits + second_row[:, None] + second_pot[None, :])
    second_col = ratio * prob
    onehot = (expert_index[:, None] == jnp.arange(experts, dtype=jnp.int32)[None, :]).astype(
        jnp.float32
    )
    direct = onehot * prob * loss_grad[:, None]
    row_direct = jnp.sum(direct, axis=1)
    second_colgrad = by_axis(jnp.sum(direct, axis=0), (("dp_0", "dp_1"), ("dp_2", "mp")))
    second_rowgrad = row_direct - jnp.dot(
        second_col, second_colgrad, precision=lax.Precision.HIGHEST
    )
    first_colgrad = by_axis(
        -jnp.sum(second_rowgrad[:, None] * second_soft, axis=0), (("dp_0", "dp_1"), ("dp_2", "mp"))
    )
    first_rowgrad = -jnp.dot(first_col, first_colgrad, precision=lax.Precision.HIGHEST)
    score_grad = (
        direct
        - second_colgrad[None, :] * second_col
        - second_rowgrad[:, None] * second_soft
        - first_colgrad[None, :] * first_col
        - first_rowgrad[:, None] * first_soft
    ).astype(jnp.bfloat16)
    score_full = collect(score_grad, "mp", 0)
    hidden_grad = lax.dot_general(
        score_full,
        whole_of(router_weight, (("dp_0", "dp_1"), "dp_2"), 0),
        (((1,), (1,)), ((), ())),
        preferred_element_type=jnp.float32,
    ).astype(jnp.bfloat16)
    weight_grad = summed_rows(
        lax.dot_general(
            hidden, score_full, (((0,), (0,)), ((), ())), preferred_element_type=jnp.float32
        ),
        (("dp_0", "dp_1"), "dp_2"),
        0,
    )
    return (weight_grad, hidden_grad)


def solution(mesh):
    split = Mesh(mesh.devices.reshape(4, 16, 2, mesh.shape["mp"]), ("dp_0", "dp_1", "dp_2", "mp"))
    return jax.shard_map(
        body,
        mesh=split,
        in_specs=(P(DP, "mp"), P(MP_DP, None), P(DP_MP, None), P(), P(), P(DP_MP), P(DP_MP)),
        out_specs=(P(MP_DP, None), P(DP, "mp")),
        check_vma=False,
    )
```

profile of v0, /device:TPU:8, one launch (start us, length us, event | category | flops | bytes accessed | tf_op | source)
XLA Modules:
  0.0 214.0 jit_solution(355945796884925441)
XLA Ops:
  0.6 1.2 fusion.15
  1.9 1.2 exponential_reduce_fusion
  3.1 1.2 fusion.5
  4.3 9.4 %all_to_all.49 = f32[8,1,256]{2,1,0:T(1,128)S(1)} all-to-all(f32[8,1,256]{2,1,0:T(1,128)S(1)} %broadcast_in_dim.14), channel_id=1, replica_groups=mesh['dp_0'=4,'dp_1'=16,'dp_2'=2,'mp'=4] {'dp_2','mp'}, dimensions={0} | all-to-all | bytes 16384 | tf_op jit(solution)/shard_map/all_to_all | solution.py:14
  13.7 32.5 %all_to_all.50 = f32[64,1,256]{2,1,0:T(1,128)S(1)} all-to-all(f32[64,1,256]{2,1,0:T(1,128)S(1)} %broadcast_in_dim.15), channel_id=1, replica_groups=mesh['dp_0'=4,'dp_1'=16,'dp_2'=2,'mp'=4] {'dp_0','dp_1'}, dimensions={0} | all-to-all | bytes 131072 | tf_op jit(solution)/shard_map/all_to_all | solution.py:14
  46.3 1.2 fusion.2
  47.6 1.1 fusion.7
  48.7 7.6 %all_to_all.51 = f32[8,1,256]{2,1,0:T(1,128)S(1)} all-to-all(f32[8,1,256]{2,1,0:T(1,128)S(1)} %broadcast_in_dim.16), channel_id=1, replica_groups=mesh['dp_0'=4,'dp_1'=16,'dp_2'=2,'mp'=4] {'dp_2','mp'}, dimensions={0} | all-to-all | bytes 16384 | tf_op jit(solution)/shard_map/all_to_all | solution.py:14
  57.0 5.5 %all-to-all-start.3 = ((f32[64,1,256]{2,1,0:T(1,128)}), f32[64,1,256]{2,1,0:T(1,128)S(1)}, u32[]{:S(2)}, u32[]{:S(2)}) async-start(f32[64,1,256]{2,1,0:T(1,128)} %broadcast_in_dim.17), calls=%async_computation.3 | async-start | bytes 131072 | tf_op jit(solution)/shard_map/all_to_all | solution.py:14
  62.6 14.2 %all-to-all-done.3 = f32[64,1,256]{2,1,0:T(1,128)S(1)} async-done(((f32[64,1,256]{2,1,0:T(1,128)}), f32[64,1,256]{2,1,0:T(1,128)S(1)}, u32[]{:S(2)}, u32[]{:S(2)}) %all-to-all-start.3) | async-done | bytes 65568 | tf_op jit(solution)/shard_map/all_to_all | solution.py:14
  76.8 1.2 fusion
  78.1 1.2 subtract_convert_fusion
  79.3 9.6 %all_to_all.52 = bf16[4,176,256]{2,1,0:T(8,128)(2,1)S(1)} all-to-all(bf16[4,176,256]{2,1,0:T(8,128)(2,1)S(1)} %broadcast_in_dim.18), channel_id=1, replica_groups=mesh['dp_0'=4,'dp_1'=16,'dp_2'=2,'mp'=4] {'mp'}, dimensions={0} | all-to-all | bytes 720896 | tf_op jit(solution)/shard_map/all_to_all | solution.py:14
  88.9 0.7 copy-done.1
  89.7 2.1 convolution_bitcast_fusion
  91.8 2.8 %copy.31 = f32[1792,256]{1,0:T(8,128)} copy(f32[1792,256]{0,1:T(8,128)} %convolution_bitcast_fusion) | data formatting | bytes 3670016 | tf_op jit(solution)/shard_map/dot_general | solution.py:111
  94.6 2.7 %reshape_reshape.6 = f32[64,2,14,256]{3,2,1,0:T(8,128)} reshape(f32[1792,256]{1,0:T(8,128)} %copy.31) | data formatting | bytes 3670016 | tf_op jit(solution)/shard_map/reshape;reshape | solution.py:49
  97.2 2.7 %copy.32 = f32[2,64,14,256]{3,1,2,0:T(8,128)S(1)} copy(f32[2,64,14,256]{3,2,0,1:T(8,128)} %bitcast.15) | data formatting | bytes 3670016 | tf_op jit(solution)/shard_map/transpose | solution.py:49
  99.9 6.1 %all_to_all.53 = f32[2,64,14,256]{3,1,2,0:T(8,128)} all-to-all(f32[2,64,14,256]{3,1,2,0:T(8,128)S(1)} %copy.32), channel_id=1, replica_groups=mesh['dp_0'=4,'dp_1'=16,'dp_2'=2,'mp'=4] {'dp_2'}, dimensions={0} | all-to-all | bytes 3670016 | tf_op jit(solution)/shard_map/all_to_all | solution.py:54
  106.0 0.8 broadcast_in_dim.19
  106.8 6.4 %all-to-all-start.7 = ((bf16[64,14,256]{2,1,0:T(8,128)(2,1)}), bf16[64,14,256]{2,1,0:T(8,128)(2,1)}, u32[]{:S(2)}, u32[]{:S(2)}) async-start(bf16[64,14,256]{2,1,0:T(8,128)(2,1)} %broadcast_in_dim.19), calls=%async_computation.7 | async-start | bytes 1048576 | tf_op jit(solution)/shard_map/all_to_all | solution.py:14
  113.2 1.7 reduce_sum.108
  114.9 1.5 copy.33
  116.4 28.9 %all-to-all-done.7 = bf16[64,14,256]{2,1,0:T(8,128)(2,1)} async-done(((bf16[64,14,256]{2,1,0:T(8,128)(2,1)}), bf16[64,14,256]{2,1,0:T(8,128)(2,1)}, u32[]{:S(2)}, u32[]{:S(2)}) %all-to-all-start.7) | async-done | bytes 458784 | tf_op jit(solution)/shard_map/all_to_all | solution.py:14
  145.4 1.2 copy.34
  146.6 4.5 %all_to_all.54 = bf16[2,64,14,256]{3,1,2,0:T(8,128)(2,1)S(1)} all-to-all(bf16[2,64,14,256]{3,1,2,0:T(8,128)(2,1)S(1)} %broadcast_in_dim.20), channel_id=1, replica_groups=mesh['dp_0'=4,'dp_1'=16,'dp_2'=2,'mp'=4] {'dp_2'}, dimensions={0} | all-to-all | bytes 1835008 | tf_op jit(solution)/shard_map/all_to_all | solution.py:14
  151.1 6.9 %all-to-all-start.6 = ((f32[64,14,256]{2,1,0:T(8,128)}), f32[64,14,256]{2,1,0:T(8,128)}, u32[]{:S(2)}, u32[]{:S(2)}) async-start(f32[64,14,256]{2,1,0:T(8,128)} %copy.33), calls=%async_computation.6 | async-start | bytes 2097152 | tf_op jit(solution)/shard_map/all_to_all | solution.py:62
  158.0 1.5 copy.35
  159.5 1.4 reshape_reshape.7
  160.9 3.3 %convolution_convert_fusion = bf16[704,1792]{1,0:T(8,128)(2,1)} fusion(bf16[704,256]{1,0:T(8,128)(2,1)} %bitcast.18, bf16[1792,256]{1,0:T(8,128)(2,1)S(1)} %reshape_reshape.7), kind=kOutput, calls=%fused_computation | convolution fusion | flops 647184384 | bytes 3801088 | tf_op jit(solution)/shard_map/dot_general | solution.py:104
  164.2 47.9 %all-to-all-done.6 = f32[64,14,256]{2,1,0:T(8,128)} async-done(((f32[64,14,256]{2,1,0:T(8,128)}), f32[64,14,256]{2,1,0:T(8,128)}, u32[]{:S(2)}, u32[]{:S(2)}) %all-to-all-start.6) | async-done | bytes 917536 | tf_op jit(solution)/shard_map/all_to_all | solution.py:62
  212.1 1.9 reduce_sum.109
  (22 shorter events, 1.2 us)
Async XLA Ops:
  0.6 89.0 %copy-start = (bf16[704,1792]{1,0:T(8,128)(2,1)S(1)}, bf16[704,1792]{1,0:T(8,128)(2,1)}, u32[]{:S(2)}) copy-start(bf16[704,1792]{1,0:T(8,128)(2,1)} %param.7) | copy-start | bytes 7569412
  57.0 19.7 %all-to-all-start.3 = ((f32[64,1,256]{2,1,0:T(1,128)}), f32[64,1,256]{2,1,0:T(1,128)S(1)}, u32[]{:S(2)}, u32[]{:S(2)}) async-start(f32[64,1,256]{2,1,0:T(1,128)} %broadcast_in_dim.17), calls=%async_computation.3 | async-start | bytes 131072 | tf_op jit(solution)/shard_map/all_to_all | solution.py:14
  88.9 0.7 copy-start.1
  99.9 6.1 %copy-start.2 = (bf16[14,256]{1,0:T(8,128)(2,1)S(1)}, bf16[14,256]{1,0:T(8,128)(2,1)}, u32[]{:S(2)}) copy-start(bf16[14,256]{1,0:T(8,128)(2,1)} %param.8) | copy-start | bytes 21508
  106.8 38.6 %all-to-all-start.7 = ((bf16[64,14,256]{2,1,0:T(8,128)(2,1)}), bf16[64,14,256]{2,1,0:T(8,128)(2,1)}, u32[]{:S(2)}, u32[]{:S(2)}) async-start(bf16[64,14,256]{2,1,0:T(8,128)(2,1)} %broadcast_in_dim.19), calls=%async_computation.7 | async-start | bytes 1048576 | tf_op jit(solution)/shard_map/all_to_all | solution.py:14
  151.1 61.0 %all-to-all-start.6 = ((f32[64,14,256]{2,1,0:T(8,128)}), f32[64,14,256]{2,1,0:T(8,128)}, u32[]{:S(2)}, u32[]{:S(2)}) async-start(f32[64,14,256]{2,1,0:T(8,128)} %copy.33), calls=%async_computation.6 | async-start | bytes 2097152 | tf_op jit(solution)/shard_map/all_to_all | solution.py:62
where the time goes:
time: 215 us; the launch traced here: 214 us
  waiting for transfers between devices  91 us (42%)
  blocking collectives  69.6 us (32%)
  starting transfers between devices  18.7 us (9%)
  local copies, waits for them, and re-layouts  16.1 us (7%)
  other arithmetic  9.84 us (5%)
  matrix products  7.91 us (4%)
    all_to_all x5, blocking collectives, copy_for_each(): lax.all_to_all(jnp.broadcast_to(array[None], (devices, *array.shape)), ax...  63.6 us
    all_to_all x1, waiting for transfers between devices, summed_rows(): lax.all_to_all(nearer, far, split_axis=0, concat_axis=0, tiled=True)  47.9 us
    all_to_all x2, waiting for transfers between devices, copy_for_each(): lax.all_to_all(jnp.broadcast_to(array[None], (devices, *array.shape)), ax...  43.1 us
    all_to_all x2, starting transfers between devices, copy_for_each(): lax.all_to_all(jnp.broadcast_to(array[None], (devices, *array.shape)), ax...  11.9 us
    all_to_all x1, starting transfers between devices, summed_rows(): lax.all_to_all(nearer, far, split_axis=0, concat_axis=0, tiled=True)  6.87 us
    all_to_all x1, blocking collectives, sum_at_owner(): lax.all_to_all(cut_along(array, dim, devices), axis, 0, 0, tiled=True)  6.06 us
  transfers between devices with their start and end apart: 3, of which 3 were waited for; matrix products, arithmetic and copies ran while one was open for 4% of the time, Pallas kernels for 0%

commit v1 on v0

v1 whole, which is shorter than its diff:
```python
import functools

import jax
import jax.numpy as jnp
from jax import lax
from jax.experimental import pallas as pl
from jax.experimental.pallas import tpu as pltpu
from jax.sharding import Mesh
from jax.sharding import PartitionSpec as P

DP = ("y", "z", "c")
F32 = jnp.float32
BF16 = jnp.bfloat16
PAD = 16


def to_each(array, axes):
    devices = lax.axis_size(axes)
    return lax.all_to_all(
        jnp.broadcast_to(array[None], (devices, *array.shape)), axes, 0, 0, tiled=True
    )


def call(kernel, out_shape, *args, flops=0, nbytes=0, name=None, **kwargs):
    return pl.pallas_call(
        kernel,
        out_shape=out_shape,
        cost_estimate=pl.CostEstimate(flops=flops, transcendentals=0, bytes_accessed=nbytes),
        name=name,
        **kwargs,
    )(*args)


def split_two(value):
    high = value.astype(BF16)
    low = (value - high.astype(F32)).astype(BF16)
    return high.astype(F32), low.astype(F32)


def as_column(row, tokens):
    shape = (tokens, row.shape[1])
    same = lax.broadcasted_iota(jnp.int32, shape, 0) == lax.broadcasted_iota(jnp.int32, shape, 1)
    return jnp.sum(jnp.where(same, row, 0.0), axis=1, keepdims=True)


def exponent_kernel(logits_ref, index_ref, grad_ref, out_ref):
    tokens, experts = logits_ref.shape
    logits = logits_ref[...]
    weight = jnp.exp(logits - jnp.max(logits, axis=1, keepdims=True))
    index = as_column(index_ref[...].astype(F32), tokens)
    lane = lax.broadcasted_iota(jnp.int32, (tokens, experts), 1).astype(F32)
    out_ref[:tokens, :] = jnp.where(lane == index, -weight, weight).astype(BF16)
    high, low = split_two(grad_ref[...])
    rows = out_ref.shape[0] - tokens
    row = lax.broadcasted_iota(jnp.int32, (rows, experts), 0)
    tail = jnp.where(row == 0, high, jnp.where(row == 1, low, 0.0))
    out_ref[tokens:, :] = tail.astype(BF16)


def tokens_of(gathered_ref, first_pot, second_pot, block, tokens):
    signed = gathered_ref[block, :tokens, :].astype(F32)
    tail = gathered_ref[block, tokens:, :].astype(F32)
    grad = as_column(tail[0:1, :] + tail[1:2, :], tokens)
    weight = jnp.abs(signed)
    first_gain = jnp.exp(first_pot)
    second_gain = jnp.exp(second_pot)
    first_scale = 1.0 / jnp.sum(weight, axis=1, keepdims=True)
    second_scale = 1.0 / jnp.sum(weight * first_gain, axis=1, keepdims=True)
    hot = jnp.where(signed < 0.0, grad, 0.0)
    return weight, first_gain, second_gain, first_scale, second_scale, hot


def direct_kernel(gathered_ref, first_ref, second_ref, router_ref, out_ref, *, tokens):
    total = 0.0
    for block in range(gathered_ref.shape[0]):
        weight, _, second_gain, _, second_scale, hot = tokens_of(
            gathered_ref, first_ref[...], second_ref[...], block, tokens
        )
        total = total + jnp.sum(weight * hot * second_scale, axis=0, keepdims=True) * second_gain
    high, low = split_two(total)
    rows, experts = router_ref.shape
    row = lax.broadcasted_iota(jnp.int32, (PAD, experts), 0)
    out_ref[:rows, :] = router_ref[...]
    out_ref[rows : rows + 1, :] = high.astype(BF16)
    out_ref[rows + 1 : rows + 2, :] = low.astype(BF16)


def along_kernel(parts_ref, out_ref, *, rows):
    members = parts_ref.shape[0]
    pair = parts_ref[:, rows : rows + 2, :].astype(F32)
    total = jnp.sum(jnp.sum(pair, axis=0), axis=0, keepdims=True)
    high, low = split_two(total)
    for member in range(1, members):
        out_ref[member * PAD : (member + 1) * PAD, :] = parts_ref[member]
    block = parts_ref[0].astype(F32)
    row = lax.broadcasted_iota(jnp.int32, block.shape, 0)
    block = jnp.where(row == rows, high, jnp.where(row == rows + 1, low, block))
    out_ref[0:PAD, :] = block.astype(BF16)


def across_kernel(parts_ref, out_ref, *, rows):
    total = 0.0
    for member in range(parts_ref.shape[0]):
        block = parts_ref[member, 0:PAD, :].astype(F32)
        total = total + jnp.sum(block[rows : rows + 2, :], axis=0, keepdims=True)
    out_ref[...] = total


def second_row_grad(token_parts, col_grad, ratio):
    weight, _, second_gain, _, second_scale, hot = token_parts
    inner = second_gain * (hot - ratio * col_grad)
    return jnp.sum(weight * inner, axis=1, keepdims=True) * second_scale, inner


def first_col_kernel(gathered_ref, first_ref, second_ref, sums_ref, out_ref, *, tokens, ratio):
    col_grad = jnp.sum(sums_ref[...], axis=0)
    total = 0.0
    for block in range(gathered_ref.shape[0]):
        parts = tokens_of(gathered_ref, first_ref[...], second_ref[...], block, tokens)
        row_grad, _ = second_row_grad(parts, col_grad, ratio)
        weight, first_gain, _, _, second_scale, _ = parts
        total = total - jnp.sum(weight * (row_grad * second_scale), axis=0, keepdims=True) * first_gain
    out_ref[...] = total


def score_kernel(
    gathered_ref,
    first_ref,
    second_ref,
    sums_ref,
    first_col_ref,
    hidden_ref,
    score_ref,
    out_ref,
    *,
    tokens,
    ratio,
):
    col_grad = jnp.sum(sums_ref[...], axis=0)
    first_col = first_col_ref[...]
    for block in range(gathered_ref.shape[0]):
        parts = tokens_of(gathered_ref, first_ref[...], second_ref[...], block, tokens)
        row_grad, inner = second_row_grad(parts, col_grad, ratio)
        weight, first_gain, _, first_scale, second_scale, _ = parts
        scaled = ratio * first_gain * first_col
        first_row = -jnp.sum(weight * scaled, axis=1, keepdims=True) * first_scale
        score = weight * (
            second_scale * (inner - first_gain * row_grad) - first_scale * (scaled + first_row)
        )
        score_ref[block * tokens : (block + 1) * tokens, :] = score.astype(BF16)
    score = score_ref[...]
    size = out_ref.shape[1]
    for part in range(out_ref.shape[0]):
        out_ref[part] = jnp.dot(
            hidden_ref[part * size : (part + 1) * size, :], score, preferred_element_type=F32
        ).astype(BF16)


def whole_part(value, size):
    return jnp.floor((value + 0.5) * (1.0 / size))


def transpose_kernel(hidden_ref, out_ref, *, along, rows):
    size = hidden_ref.shape[1]
    target = lax.broadcasted_iota(jnp.int32, (size, size), 0).astype(F32)
    source = lax.broadcasted_iota(jnp.int32, (size, size), 1).astype(F32)
    span = along * rows
    outer = whole_part(target, 2 * span)
    rest = target - outer * (2 * span)
    core = whole_part(rest, span)
    rest = rest - core * span
    place = whole_part(rest, rows)
    wanted = outer * (2 * span) + place * (2 * rows) + core * rows + (rest - place * rows)
    order = jnp.where(source == wanted, 1.0, 0.0).astype(BF16)
    out_ref[...] = lax.dot_general(
        order, hidden_ref[...], (((1,), (1,)), ((), ())), preferred_element_type=F32
    ).astype(BF16)


def near_kernel(parts_ref, out_ref, *, along, rows):
    total = 0.0
    for member in range(parts_ref.shape[0]):
        total = total + parts_ref[member].astype(F32)
    for place in range(along):
        out_ref[place] = total[place * rows : (place + 1) * rows, :].astype(BF16)


def far_kernel(parts_ref, out_ref):
    total = 0.0
    for member in range(parts_ref.shape[0]):
        total = total + parts_ref[member].astype(F32)
    out_ref[...] = total


def hidden_kernel(core_ref, score_ref, mine_ref, other_ref, out_ref, router_ref, *, rows):
    members, padded, _ = mine_ref.shape
    along = padded // PAD
    size = 2 * along * rows

    @pl.when(pl.program_id(0) == 0)
    def _():
        target = lax.broadcasted_iota(jnp.int32, (size, padded), 0).astype(F32)
        column = lax.broadcasted_iota(jnp.int32, (size, padded), 1).astype(F32)
        place = whole_part(column, PAD)
        row = column - place * PAD
        base = place * (2 * rows) + row
        kept = row < rows
        mine_at = core_ref[0].astype(F32) * rows
        mine = jnp.where(kept & (target == base + mine_at), 1.0, 0.0).astype(BF16)
        other = jnp.where(kept & (target == base + (rows - mine_at)), 1.0, 0.0).astype(BF16)
        for member in range(members):
            whole = jnp.dot(mine, mine_ref[member], preferred_element_type=F32) + jnp.dot(
                other, other_ref[member], preferred_element_type=F32
            )
            router_ref[member * size : (member + 1) * size, :] = whole.astype(BF16)

    width = out_ref.shape[1]
    start = pl.multiple_of(pl.program_id(0) * width, width)
    out_ref[...] = lax.dot_general(
        score_ref[...],
        router_ref[pl.ds(start, width), :],
        (((1,), (1,)), ((), ())),
        preferred_element_type=F32,
    ).astype(BF16)


def body(hidden, router_weight, logits, first_pot, second_pot, expert_index, loss_grad):
    tokens, experts = logits.shape
    rows = router_weight.shape[0]
    across, along = lax.axis_size("y"), lax.axis_size("z")
    blocks = lax.axis_size("x")
    ratio = experts / (tokens * blocks * lax.axis_size(DP))
    all_tokens, width = hidden.shape
    vmem = pl.BlockSpec(memory_space=pltpu.VMEM)

    padding = ((0, 0), (0, experts - tokens))
    exponents = call(
        exponent_kernel,
        jax.ShapeDtypeStruct((tokens + PAD, experts), BF16),
        logits,
        jnp.pad(expert_index[None], padding),
        jnp.pad(loss_grad[None], padding),
        name="exponents",
    )
    gathered = to_each(exponents, "x")
    pots = (first_pot[None], second_pot[None])

    half = across * along * 2 * rows // max(across // 2, 1)
    transposed = call(
        functools.partial(transpose_kernel, along=along, rows=rows),
        jax.ShapeDtypeStruct((width, all_tokens), BF16),
        hidden,
        grid=(width // half,),
        in_specs=[pl.BlockSpec((all_tokens, half), lambda i: (0, i))],
        out_specs=pl.BlockSpec((half, all_tokens), lambda i: (i, 0)),
        flops=2 * width * half * all_tokens,
        nbytes=4 * width * all_tokens,
        name="transposed",
    )

    sent = call(
        functools.partial(direct_kernel, tokens=tokens),
        jax.ShapeDtypeStruct((PAD, experts), BF16),
        gathered,
        *pots,
        router_weight,
        name="direct",
    )
    along_parts = to_each(sent, "z")
    sent = call(
        functools.partial(along_kernel, rows=rows),
        jax.ShapeDtypeStruct((along * PAD, experts), BF16),
        along_parts,
        name="along",
    )
    across_parts = to_each(sent, "y")
    sent = call(
        functools.partial(across_kernel, rows=rows),
        jax.ShapeDtypeStruct((1, experts), F32),
        across_parts,
        name="across",
    )
    sums = to_each(sent, "c")
    other_router = lax.ppermute(across_parts, "c", [(0, 1), (1, 0)])

    partial_col = call(
        functools.partial(first_col_kernel, tokens=tokens, ratio=ratio),
        jax.ShapeDtypeStruct((1, experts), F32),
        gathered,
        *pots,
        sums,
        name="first_col",
    )
    first_col = jnp.sum(to_each(partial_col, DP), axis=0)

    score, products = call(
        functools.partial(score_kernel, tokens=tokens, ratio=ratio),
        (
            jax.ShapeDtypeStruct((all_tokens, experts), BF16),
            jax.ShapeDtypeStruct((2 * across, along * rows, experts), BF16),
        ),
        gathered,
        *pots,
        sums,
        first_col,
        transposed,
        flops=2 * all_tokens * width * experts,
        nbytes=2 * all_tokens * width,
        name="score",
    )
    near = lax.all_to_all(products, ("y", "c"), 0, 0, tiled=True)
    far = call(
        functools.partial(near_kernel, along=along, rows=rows),
        jax.ShapeDtypeStruct((along, rows, experts), BF16),
        near,
        name="near",
    )
    far = lax.all_to_all(far, "z", 0, 0, tiled=True)

    chunk = 256 if width % 256 == 0 else width
    hidden_grad = call(
        functools.partial(hidden_kernel, rows=rows),
        jax.ShapeDtypeStruct((all_tokens, width), BF16),
        lax.axis_index("c").astype(jnp.int32)[None],
        score,
        across_parts,
        other_router,
        grid=(width // chunk,),
        in_specs=[
            pl.BlockSpec(memory_space=pltpu.SMEM),
            vmem,
            vmem,
            vmem,
        ],
        out_specs=pl.BlockSpec((all_tokens, chunk), lambda i: (0, i)),
        scratch_shapes=[pltpu.VMEM((width, experts), BF16)],
        flops=2 * all_tokens * width * experts,
        nbytes=2 * all_tokens * width,
        name="hidden_grad",
    )
    weight_grad = call(
        far_kernel, jax.ShapeDtypeStruct((rows, experts), F32), far, name="weight_grad"
    )
    return weight_grad, hidden_grad


def solution(mesh):
    dp, mp = mesh.devices.shape
    along = dp // 8
    split = Mesh(mesh.devices.reshape(4, along, 2, mp), ("y", "z", "c", "x"))
    token_rows = ("y", "z", "c", "x")
    weight_rows = ("x", "y", "z", "c")
    return jax.shard_map(
        body,
        mesh=split,
        in_specs=(
            P(DP, "x"),
            P(weight_rows, None),
            P(token_rows, None),
            P(),
            P(),
            P(token_rows),
            P(token_rows),
        ),
        out_specs=(P(weight_rows, None), P(DP, "x")),
        check_vma=False,
    )
```

time: 215 us -> 146 us (0.68)
  the two profiles are of different devices: /device:TPU:8 before, /device:TPU:32 now
where the time goes in v1:
time: 146 us; the launch traced here: 145 us
  blocking collectives  57 us (39%)
  waiting for transfers between devices  30.9 us (21%)
  Pallas kernels  28.9 us (20%)
  starting transfers between devices  17.2 us (12%)
  local copies, waits for them, and re-layouts  9.49 us (6%)
    all_to_all x4, blocking collectives, to_each(): lax.all_to_all(jnp.broadcast_to(array[None], (devices, *array.shape)), ax...  57 us
    pallas_call x10, Pallas kernels, call(): pl.pallas_call(kernel, out_shape=out_shape, cost_estimate=pl.CostEstimate...  28.9 us
    all_to_all x1, waiting for transfers between devices, body(): near = lax.all_to_all(products, ('y', 'c'), 0, 0, tiled=True)  12.1 us
    all_to_all x1, waiting for transfers between devices, to_each(): lax.all_to_all(jnp.broadcast_to(array[None], (devices, *array.shape)), ax...  11.6 us
    all_to_all x1, waiting for transfers between devices, body(): far = lax.all_to_all(far, 'z', 0, 0, tiled=True)  7.16 us
    all_to_all x1, starting transfers between devices, to_each(): lax.all_to_all(jnp.broadcast_to(array[None], (devices, *array.shape)), ax...  6.61 us
    all_to_all x1, starting transfers between devices, body(): far = lax.all_to_all(far, 'z', 0, 0, tiled=True)  4.72 us
    broadcast_in_dim x5, local copies, waits for them, and re-layouts, to_each(): jnp.broadcast_to(array[None], (devices, *array.shape))  4.64 us
  transfers between devices with their start and end apart: 4, of which 3 were waited for; matrix products, arithmetic and copies ran while one was open for 0% of the time, Pallas kernels for 10%

profile of v1, /device:TPU:32, one launch (start us, length us, event | category | flops | bytes accessed | tf_op | source)
XLA Modules:
  0.0 144.9 jit_solution(449211153104129064)
XLA Ops:
  0.6 1.2 pad.8.index_ref
  1.9 1.2 pad.9.grad_ref
  3.1 1.7 %exponents.1 = bf16[192,256]{1,0:T(8,128)(2,1)} custom-call(f32[176,256]{1,0:T(8,128)} %logits_ref.1, s32[1,256]{1,0:T(1,128)} %pad.8.index_ref, f32[1,256]{1,0:T(1,128)} %pad.9.grad_ref), custom_call_target="tpu_custom_call" | custom-call | tf_op jit(solution)/shard_map/exponents/pallas_call | solution.py:25
  4.8 0.9 broadcast_in_dim.51
  5.7 12.3 %all_to_all.35.gathered_ref = bf16[4,192,256]{2,1,0:T(8,128)(2,1)} all-to-all(bf16[4,192,256]{2,1,0:T(8,128)(2,1)S(1)} %broadcast_in_dim.51), channel_id=1, replica_groups=mesh['y'=4,'z'=16,'c'=2,'x'=4] {'x'}, dimensions={0} | all-to-all | bytes 786432 | tf_op jit(solution)/shard_map/all_to_all | solution.py:19
  18.0 1.9 %direct.1 = bf16[16,256]{1,0:T(8,128)(2,1)} custom-call(bf16[4,192,256]{2,1,0:T(8,128)(2,1)} %all_to_all.35.gathered_ref, f32[1,256]{1,0:T(1,128)} %bitcast.8, f32[1,256]{1,0:T(1,128)} %bitcast.11, bf16[14,256]{1,0:T(8,128)(2,1)} %router_ref.1), custom_call_target="tpu_custom_call" | custom-call | tf_op jit(solution)/shard_map/direct/pallas_call | solution.py:25
  20.0 0.7 broadcast_in_dim.54
  20.7 27.9 %all_to_all.36.parts_ref = bf16[16,16,256]{2,1,0:T(8,128)(2,1)} all-to-all(bf16[16,16,256]{2,1,0:T(8,128)(2,1)S(1)} %broadcast_in_dim.54), channel_id=1, replica_groups=mesh['y'=4,'z'=16,'c'=2,'x'=4] {'z'}, dimensions={0} | all-to-all | bytes 262144 | tf_op jit(solution)/shard_map/all_to_all | solution.py:19
  48.5 1.6 %along.1 = bf16[256,256]{1,0:T(8,128)(2,1)} custom-call(bf16[16,16,256]{2,1,0:T(8,128)(2,1)} %all_to_all.36.parts_ref), custom_call_target="tpu_custom_call" | custom-call | tf_op jit(solution)/shard_map/along/pallas_call | solution.py:25
  50.1 0.9 broadcast_in_dim.55
  51.1 12.5 %all_to_all.37.parts_ref.mine_ref = bf16[4,256,256]{2,1,0:T(8,128)(2,1)} all-to-all(bf16[4,256,256]{2,1,0:T(8,128)(2,1)S(1)} %broadcast_in_dim.55), channel_id=1, replica_groups=mesh['y'=4,'z'=16,'c'=2,'x'=4] {'y'}, dimensions={0} | all-to-all | bytes 1048576 | tf_op jit(solution)/shard_map/all_to_all | solution.py:19
  63.5 1.6 %across.1 = f32[1,256]{1,0:T(1,128)} custom-call(bf16[4,256,256]{2,1,0:T(8,128)(2,1)} %all_to_all.37.parts_ref.mine_ref), custom_call_target="tpu_custom_call" | custom-call | tf_op jit(solution)/shard_map/across/pallas_call | solution.py:25
  65.1 0.7 broadcast_in_dim.57
  65.8 4.4 %all_to_all.38.sums_ref = f32[2,1,256]{2,1,0:T(1,128)} all-to-all(f32[2,1,256]{2,1,0:T(1,128)S(1)} %broadcast_in_dim.57), channel_id=1, replica_groups=mesh['y'=4,'z'=16,'c'=2,'x'=4] {'c'}, dimensions={0} | all-to-all | bytes 4096 | tf_op jit(solution)/shard_map/all_to_all | solution.py:19
  70.2 2.1 %first_col.1 = f32[1,256]{1,0:T(1,128)} custom-call(bf16[4,192,256]{2,1,0:T(8,128)(2,1)} %all_to_all.35.gathered_ref, f32[1,256]{1,0:T(1,128)} %bitcast.9, f32[1,256]{1,0:T(1,128)} %bitcast.12, f32[2,1,256]{2,1,0:T(1,128)} %all_to_all.38.sums_ref), custom_call_target="tpu_custom_call" | custom-call | tf_op jit(solution)/shard_map/first_col/pallas_call | solution.py:25
  72.3 1.4 broadcast_in_dim.59
  73.7 6.6 %all-to-all-start.4 = ((f32[128,1,256]{2,1,0:T(1,128)}), f32[128,1,256]{2,1,0:T(1,128)S(1)}, u32[]{:S(2)}, u32[]{:S(2)}) async-start(f32[128,1,256]{2,1,0:T(1,128)} %broadcast_in_dim.59), calls=%async_computation.4 | async-start | bytes 262144 | tf_op jit(solution)/shard_map/all_to_all | solution.py:19
  80.3 6.1 %transposed.1.hidden_ref = bf16[1792,704]{1,0:T(8,128)(2,1)} custom-call(bf16[704,1792]{1,0:T(8,128)(2,1)} %hidden_ref.1), custom_call_target="tpu_custom_call" | custom-call | flops 2260729856 | bytes 5046272 | tf_op jit(solution)/shard_map/transposed/pallas_call | solution.py:25
  86.3 11.6 %all-to-all-done.4 = f32[128,1,256]{2,1,0:T(1,128)S(1)} async-done(((f32[128,1,256]{2,1,0:T(1,128)}), f32[128,1,256]{2,1,0:T(1,128)S(1)}, u32[]{:S(2)}, u32[]{:S(2)}) %all-to-all-start.4) | async-done | bytes 131104 | tf_op jit(solution)/shard_map/all_to_all | solution.py:19
  98.0 0.7 reduce_sum.11
  98.7 4.3 %score.1 = (bf16[704,256]{1,0:T(8,128)(2,1)}, bf16[8,224,256]{2,1,0:T(8,128)(2,1)}) custom-call(bf16[4,192,256]{2,1,0:T(8,128)(2,1)} %all_to_all.35.gathered_ref, f32[1,256]{1,0:T(1,128)} %bitcast.10, f32[1,256]{1,0:T(1,128)} %bitcast.13, f32[2,1,256]{2,1,0:T(1,128)} %all_to_all.38.sums_ref, f32[1,256]{1,0:T(1,128)} %bitcast.14, ...), custom_call_target="tpu_custom_call" | custom-call | flops 645922816 | bytes 2523136 | tf_op jit(solution)/shard_map/score/pallas_call | solution.py:25
  103.0 3.6 %all-to-all-start.5 = ((bf16[8,224,256]{2,1,0:T(8,128)(2,1)}), bf16[8,224,256]{2,1,0:T(8,128)(2,1)S(1)}, u32[]{:S(2)}, u32[]{:S(2)}) async-start(bf16[8,224,256]{2,1,0:T(8,128)(2,1)} %get-tuple-element.4), calls=%async_computation.5 | async-start | bytes 1835008 | tf_op jit(solution)/shard_map/all_to_all | solution.py:311
  106.6 2.3 %collective-permute-start = (bf16[4,256,256]{2,1,0:T(8,128)(2,1)S(1)}, bf16[4,256,256]{2,1,0:T(8,128)(2,1)S(1)}, u32[]{:S(2)}, u32[]{:S(2)}) collective-permute-start(bf16[4,256,256]{2,1,0:T(8,128)(2,1)S(1)} %copy-done), channel_id=1, source_target_pairs={{0,4},{4,0},{1,5},{5,1},{2,6},{6,2},{3,7},{7,3},{8,12},{12,8},{9,1... | collective-permute-start | bytes 1572872 | tf_op jit(solution)/shard_map/ppermute | solution.py:284
  108.9 12.1 %all-to-all-done.5.parts_ref = bf16[8,224,256]{2,1,0:T(8,128)(2,1)S(1)} async-done(((bf16[8,224,256]{2,1,0:T(8,128)(2,1)}), bf16[8,224,256]{2,1,0:T(8,128)(2,1)S(1)}, u32[]{:S(2)}, u32[]{:S(2)}) %all-to-all-start.5) | async-done | bytes 917536 | tf_op jit(solution)/shard_map/all_to_all | solution.py:311
  121.1 0.9 copy-done.1
  122.0 2.0 %near.1 = bf16[16,14,256]{2,1,0:T(8,128)(2,1)} custom-call(bf16[8,224,256]{2,1,0:T(8,128)(2,1)} %copy-done.1), custom_call_target="tpu_custom_call" | custom-call | tf_op jit(solution)/shard_map/near/pallas_call | solution.py:25
  124.0 4.7 %all-to-all-start.6 = ((bf16[16,14,256]{2,1,0:T(8,128)(2,1)}), bf16[16,14,256]{2,1,0:T(8,128)(2,1)S(1)}, u32[]{:S(2)}, u32[]{:S(2)}) async-start(bf16[16,14,256]{2,1,0:T(8,128)(2,1)} %near.1), calls=%async_computation.6 | async-start | bytes 262144 | tf_op jit(solution)/shard_map/all_to_all | solution.py:318
  128.7 0.8 copy-done.2
  129.5 6.1 %hidden_grad.1 = bf16[704,1792]{1,0:T(8,128)(2,1)} custom-call(s32[1]{0:T(128)} %bitcast.7.core_ref, bf16[704,256]{1,0:T(8,128)(2,1)} %get-tuple-element.5.score_ref, bf16[4,256,256]{2,1,0:T(8,128)(2,1)} %all_to_all.37.parts_ref.mine_ref, bf16[4,256,256]{2,1,0:T(8,128)(2,1)} %copy-done.2), custom_call_target="tpu_custom_call" | custom-call | flops 645922816 | bytes 2523136 | tf_op jit(solution)/shard_map/hidden_grad/pallas_call | solution.py:25
  135.5 7.2 %all-to-all-done.6.parts_ref = bf16[16,14,256]{2,1,0:T(8,128)(2,1)S(1)} async-done(((bf16[16,14,256]{2,1,0:T(8,128)(2,1)}), bf16[16,14,256]{2,1,0:T(8,128)(2,1)S(1)}, u32[]{:S(2)}, u32[]{:S(2)}) %all-to-all-start.6) | async-done | bytes 114720 | tf_op jit(solution)/shard_map/all_to_all | solution.py:318
  142.7 0.6 copy-done.3
  143.3 1.5 %weight_grad.1 = f32[14,256]{1,0:T(8,128)} custom-call(bf16[16,14,256]{2,1,0:T(8,128)(2,1)} %copy-done.3), custom_call_target="tpu_custom_call" | custom-call | tf_op jit(solution)/shard_map/weight_grad/pallas_call | solution.py:25
  (6 shorter events, 0.0 us)
Async XLA Ops:
  73.7 24.3 %all-to-all-start.4 = ((f32[128,1,256]{2,1,0:T(1,128)}), f32[128,1,256]{2,1,0:T(1,128)S(1)}, u32[]{:S(2)}, u32[]{:S(2)}) async-start(f32[128,1,256]{2,1,0:T(1,128)} %broadcast_in_dim.59), calls=%async_computation.4 | async-start | bytes 262144 | tf_op jit(solution)/shard_map/all_to_all | solution.py:19
  98.7 7.9 %copy-start = (bf16[4,256,256]{2,1,0:T(8,128)(2,1)S(1)}, bf16[4,256,256]{2,1,0:T(8,128)(2,1)}, u32[]{:S(2)}) copy-start(bf16[4,256,256]{2,1,0:T(8,128)(2,1)} %all_to_all.37.parts_ref.mine_ref) | copy-start | bytes 1572868
  103.0 18.0 %all-to-all-start.5 = ((bf16[8,224,256]{2,1,0:T(8,128)(2,1)}), bf16[8,224,256]{2,1,0:T(8,128)(2,1)S(1)}, u32[]{:S(2)}, u32[]{:S(2)}) async-start(bf16[8,224,256]{2,1,0:T(8,128)(2,1)} %get-tuple-element.4), calls=%async_computation.5 | async-start | bytes 1835008 | tf_op jit(solution)/shard_map/all_to_all | solution.py:311
  106.6 22.1 %collective-permute-start = (bf16[4,256,256]{2,1,0:T(8,128)(2,1)S(1)}, bf16[4,256,256]{2,1,0:T(8,128)(2,1)S(1)}, u32[]{:S(2)}, u32[]{:S(2)}) collective-permute-start(bf16[4,256,256]{2,1,0:T(8,128)(2,1)S(1)} %copy-done), channel_id=1, source_target_pairs={{0,4},{4,0},{1,5},{5,1},{2,6},{6,2},{3,7},{7,3},{8,12},{12,8},{9,1... | collective-permute-start | bytes 1572872 | tf_op jit(solution)/shard_map/ppermute | solution.py:284
  121.1 0.9 copy-start.1
  124.0 18.7 %all-to-all-start.6 = ((bf16[16,14,256]{2,1,0:T(8,128)(2,1)}), bf16[16,14,256]{2,1,0:T(8,128)(2,1)S(1)}, u32[]{:S(2)}, u32[]{:S(2)}) async-start(bf16[16,14,256]{2,1,0:T(8,128)(2,1)} %near.1), calls=%async_computation.6 | async-start | bytes 262144 | tf_op jit(solution)/shard_map/all_to_all | solution.py:318
  128.7 0.8 copy-start.2
  142.7 0.6 copy-start.3

commit v2 on v1

v2 whole, which is shorter than its diff:
```python
import functools

import jax
import jax.numpy as jnp
from jax import lax
from jax.experimental import pallas as pl
from jax.experimental.pallas import tpu as pltpu
from jax.sharding import Mesh
from jax.sharding import PartitionSpec as P

DP = ("y", "z", "c")
F32 = jnp.float32
BF16 = jnp.bfloat16
PAD = 16


def kept(shape, dtype):
    return pltpu.VMEM(shape, dtype)


def placed(array, near):
    return pltpu.with_memory_space_constraint(array, pltpu.VMEM if near else pltpu.HBM)


def call(kernel, shapes, *args, far=(), flops=0, nbytes=0, limit=16, name=None, **kwargs):
    return pl.pallas_call(
        kernel,
        out_shape=shapes,
        cost_estimate=pl.CostEstimate(flops=flops, transcendentals=0, bytes_accessed=nbytes),
        name=name,
        compiler_params=pltpu.CompilerParams(vmem_limit_bytes=limit << 20),
        **kwargs,
    )(*(placed(arg, at not in far) for at, arg in enumerate(args)))


def split_two(value):
    high = value.astype(BF16)
    low = (value - high.astype(F32)).astype(BF16)
    return high.astype(F32), low.astype(F32)


def as_column(row, tokens):
    shape = (tokens, row.shape[1])
    same = lax.broadcasted_iota(jnp.int32, shape, 0) == lax.broadcasted_iota(jnp.int32, shape, 1)
    return jnp.sum(jnp.where(same, row, 0.0), axis=1, keepdims=True)


def exponent_kernel(
    logits_ref, index_ref, grad_ref, first_ref, second_ref, router_ref, out_ref, gains_ref, copy_ref
):
    tokens, experts = logits_ref.shape
    logits = logits_ref[...]
    weight = jnp.exp(logits - jnp.max(logits, axis=1, keepdims=True))
    index = as_column(index_ref[...].astype(F32), tokens)
    lane = lax.broadcasted_iota(jnp.int32, (tokens, experts), 1).astype(F32)
    out_ref[:tokens, :] = jnp.where(lane == index, -weight, weight).astype(BF16)
    high, low = split_two(grad_ref[...])
    rows = out_ref.shape[0] - tokens
    out_ref[tokens:, :] = jnp.zeros((rows, experts), BF16)
    row = lax.broadcasted_iota(jnp.int32, (rows, tokens), 0)
    tail = jnp.where(row == 0, high, jnp.where(row == 1, low, 0.0))
    out_ref[tokens:, :tokens] = tail.astype(BF16)
    gains_ref[0:1, :] = jnp.exp(first_ref[...])
    gains_ref[1:2, :] = jnp.exp(second_ref[...])
    copy_ref[...] = router_ref[...]


def tokens_of(gathered_ref, gains_ref, block, tokens):
    signed = gathered_ref[block, :tokens, :].astype(F32)
    tail = gathered_ref[block, tokens:, :].astype(F32)
    grad = as_column(tail[0:1, :] + tail[1:2, :], tokens)
    weight = jnp.abs(signed)
    second_scale = 1.0 / jnp.sum(weight * gains_ref[0:1, :], axis=1, keepdims=True)
    hot = jnp.where(signed < 0.0, grad, 0.0)
    return weight, second_scale, hot


def direct_kernel(gathered_ref, gains_ref, router_ref, out_ref, *, tokens):
    total = 0.0
    for block in range(gathered_ref.shape[0]):
        weight, second_scale, hot = tokens_of(gathered_ref, gains_ref, block, tokens)
        total = total + jnp.sum(weight * hot * second_scale, axis=0, keepdims=True)
    high, low = split_two(total * gains_ref[1:2, :])
    rows = router_ref.shape[0]
    for member in range(out_ref.shape[0]):
        out_ref[member, :rows, :] = router_ref[...]
        out_ref[member, rows : rows + 1, :] = high.astype(BF16)
        out_ref[member, rows + 1 : rows + 2, :] = low.astype(BF16)


def prepare_kernel(gathered_ref, gains_ref, direct_ref, prob_ref, soft_ref, *, tokens):
    for block in range(gathered_ref.shape[0]):
        weight, second_scale, hot = tokens_of(gathered_ref, gains_ref, block, tokens)
        here = slice(block * tokens, (block + 1) * tokens)
        prob = weight * gains_ref[1:2, :] * second_scale
        prob_ref[here, :] = prob
        direct_ref[here, :] = prob * hot
        soft_ref[here, :] = weight * gains_ref[0:1, :] * second_scale


def along_kernel(parts_ref, out_ref, *, rows):
    members = parts_ref.shape[0]
    pair = parts_ref[:, rows : rows + 2, :].astype(F32)
    total = jnp.sum(jnp.sum(pair, axis=0), axis=0, keepdims=True)
    high, low = split_two(total)
    for member in range(1, members):
        out_ref[member * PAD : (member + 1) * PAD, :] = parts_ref[member]
    block = parts_ref[0].astype(F32)
    row = lax.broadcasted_iota(jnp.int32, block.shape, 0)
    block = jnp.where(row == rows, high, jnp.where(row == rows + 1, low, block))
    out_ref[0:PAD, :] = block.astype(BF16)


def across_kernel(parts_ref, out_ref, *, rows):
    total = 0.0
    for member in range(parts_ref.shape[0]):
        block = parts_ref[member, 0:PAD, :].astype(F32)
        total = total + jnp.sum(block[rows : rows + 2, :], axis=0, keepdims=True)
    out_ref[...] = total


def second_row_grad(direct, prob, scaled):
    return jnp.sum(direct - prob * scaled, axis=1, keepdims=True)


def first_col_kernel(direct_ref, prob_ref, soft_ref, sums_ref, out_ref, *, ratio):
    scaled = ratio * jnp.sum(sums_ref[...], axis=0)
    row_grad = second_row_grad(direct_ref[...], prob_ref[...], scaled)
    total = -jnp.sum(soft_ref[...] * row_grad, axis=0, keepdims=True)
    for member in range(out_ref.shape[0]):
        out_ref[member] = total


def second_kernel(gathered_ref, gains_ref, sums_ref, out_ref, first_ref, *, ratio, tokens):
    scaled = ratio * jnp.sum(sums_ref[...], axis=0)
    for block in range(gathered_ref.shape[0]):
        weight, second_scale, hot = tokens_of(gathered_ref, gains_ref, block, tokens)
        here = slice(block * tokens, (block + 1) * tokens)
        left = weight * second_scale * (gains_ref[1:2, :] * (hot - scaled))
        row = jnp.sum(left, axis=1, keepdims=True)
        out_ref[here, :] = left - weight * gains_ref[0:1, :] * (second_scale * row)
        first_ref[here, :] = weight * (1.0 / jnp.sum(weight, axis=1, keepdims=True))


def score_kernel(
    second_ref,
    first_ref,
    gains_ref,
    first_col_ref,
    hidden_ref,
    score_ref,
    out_ref,
    near_ref,
    done_ref,
    *,
    ratio,
):
    parts, size, _ = out_ref.shape
    copies = []
    for part in range(parts):
        here = pl.ds(part * size, size)
        copies.append(
            pltpu.make_async_copy(hidden_ref.at[here], near_ref.at[here], done_ref.at[part])
        )
        copies[part].start()
    scaled = ratio * gains_ref[0:1, :] * jnp.sum(first_col_ref[...], axis=0)
    first = first_ref[...]
    row = jnp.sum(first * scaled, axis=1, keepdims=True)
    score = (second_ref[...] - first * (scaled - row)).astype(BF16)
    score_ref[...] = score
    for part in range(parts):
        copies[part].wait()
        out_ref[part] = jnp.dot(
            near_ref[part * size : (part + 1) * size, :],
            score_ref[...],
            preferred_element_type=F32,
        ).astype(BF16)


def whole_part(value, size):
    return jnp.floor((value + 0.5) * (1.0 / size))


def transpose_kernel(hidden_ref, out_ref, *, along, rows):
    span = along * rows
    size = 4 * span if out_ref.shape[0] % (4 * span) == 0 else 2 * span
    target = lax.broadcasted_iota(jnp.int32, (size, size), 0).astype(F32)
    source = lax.broadcasted_iota(jnp.int32, (size, size), 1).astype(F32)
    outer = whole_part(target, 2 * span)
    rest = target - outer * (2 * span)
    core = whole_part(rest, span)
    rest = rest - core * span
    place = whole_part(rest, rows)
    wanted = outer * (2 * span) + place * (2 * rows) + core * rows + (rest - place * rows)
    order = jnp.where(source == wanted, 1.0, 0.0).astype(BF16)
    for start in range(0, out_ref.shape[0], size):
        out_ref[start : start + size, :] = lax.dot_general(
            order,
            hidden_ref[:, start : start + size],
            (((1,), (1,)), ((), ())),
            preferred_element_type=F32,
        ).astype(BF16)


def near_kernel(parts_ref, out_ref, *, along, rows):
    total = 0.0
    for member in range(parts_ref.shape[0]):
        total = total + parts_ref[member].astype(F32)
    for place in range(along):
        out_ref[place] = total[place * rows : (place + 1) * rows, :].astype(BF16)


def far_kernel(parts_ref, out_ref):
    total = 0.0
    for member in range(parts_ref.shape[0]):
        total = total + parts_ref[member].astype(F32)
    out_ref[...] = total


def hidden_kernel(core_ref, score_ref, mine_ref, other_ref, out_ref, router_ref, *, rows):
    members, padded, _ = mine_ref.shape
    along = padded // PAD
    size = 2 * along * rows

    @pl.when(pl.program_id(0) == 0)
    def _():
        target = lax.broadcasted_iota(jnp.int32, (size, padded), 0).astype(F32)
        column = lax.broadcasted_iota(jnp.int32, (size, padded), 1).astype(F32)
        place = whole_part(column, PAD)
        row = column - place * PAD
        base = place * (2 * rows) + row
        kept = row < rows
        mine_at = core_ref[0].astype(F32) * rows
        mine = jnp.where(kept & (target == base + mine_at), 1.0, 0.0).astype(BF16)
        other = jnp.where(kept & (target == base + (rows - mine_at)), 1.0, 0.0).astype(BF16)
        for member in range(members):
            whole = jnp.dot(mine, mine_ref[member], preferred_element_type=F32) + jnp.dot(
                other, other_ref[member], preferred_element_type=F32
            )
            router_ref[member * size : (member + 1) * size, :] = whole.astype(BF16)

    width = out_ref.shape[1]
    start = pl.multiple_of(pl.program_id(0) * width, width)
    out_ref[...] = lax.dot_general(
        score_ref[...],
        router_ref[pl.ds(start, width), :],
        (((1,), (1,)), ((), ())),
        preferred_element_type=F32,
    ).astype(BF16)


def body(hidden, router_weight, logits, first_pot, second_pot, expert_index, loss_grad):
    tokens, experts = logits.shape
    rows = router_weight.shape[0]
    across, along = lax.axis_size("y"), lax.axis_size("z")
    blocks = lax.axis_size("x")
    ratio = experts / (tokens * blocks * lax.axis_size(DP))
    all_tokens, width = hidden.shape
    vmem = pl.BlockSpec(memory_space=pltpu.VMEM)
    exponents, gains, router = call(
        exponent_kernel,
        (
            kept((tokens + PAD, experts), BF16),
            kept((2, experts), F32),
            kept((rows, experts), BF16),
        ),
        logits,
        expert_index[None],
        loss_grad[None],
        first_pot[None],
        second_pot[None],
        router_weight,
        far=range(6),
        name="exponents",
    )
    gathered = lax.all_gather(exponents, "x")
    whole = (all_tokens, experts)

    transposed = call(
        functools.partial(transpose_kernel, along=along, rows=rows),
        jax.ShapeDtypeStruct((width, all_tokens), BF16),
        hidden,
        far=(0,),
        in_specs=[vmem],
        out_specs=vmem,
        flops=width * width * all_tokens,
        nbytes=4 * width * all_tokens,
        limit=32,
        name="transposed",
    )

    sent = call(
        functools.partial(direct_kernel, tokens=tokens),
        jax.ShapeDtypeStruct((along, PAD, experts), BF16),
        gathered,
        gains,
        router,
        name="direct",
    )
    along_parts = lax.all_to_all(sent, "z", 0, 0, tiled=True)
    direct, prob, soft = call(
        functools.partial(prepare_kernel, tokens=tokens),
        (kept(whole, F32),) * 3,
        gathered,
        gains,
        flops=40 * all_tokens * experts,
        nbytes=14 * all_tokens * experts,
        name="prepared",
    )
    sent = call(
        functools.partial(along_kernel, rows=rows),
        kept((along * PAD, experts), BF16),
        along_parts,
        name="along",
    )
    across_parts = lax.all_gather(sent, "y")
    sent = call(
        functools.partial(across_kernel, rows=rows),
        kept((1, experts), F32),
        across_parts,
        name="across",
    )
    sums = lax.all_gather(sent, "c")
    other_router = lax.ppermute(across_parts, "c", [(0, 1), (1, 0)])

    partial_col = call(
        functools.partial(first_col_kernel, ratio=ratio),
        jax.ShapeDtypeStruct((lax.axis_size(DP), 1, experts), F32),
        direct,
        prob,
        soft,
        sums,
        name="first_col",
    )
    first_col = lax.all_to_all(partial_col, DP, 0, 0, tiled=True)
    second, first = call(
        functools.partial(second_kernel, ratio=ratio, tokens=tokens),
        (kept(whole, F32), kept(whole, F32)),
        gathered,
        gains,
        sums,
        flops=40 * all_tokens * experts,
        nbytes=10 * all_tokens * experts,
        name="second",
    )

    parts = 2 * across
    score, products = call(
        functools.partial(score_kernel, ratio=ratio),
        (
            kept(whole, BF16),
            jax.ShapeDtypeStruct((parts, along * rows, experts), BF16),
        ),
        second,
        first,
        gains,
        first_col,
        transposed,
        far=(4,),
        in_specs=[vmem] * 4 + [pl.BlockSpec(memory_space=pl.ANY)],
        out_specs=(vmem, vmem),
        scratch_shapes=[
            pltpu.VMEM((width, all_tokens), BF16),
            pltpu.SemaphoreType.DMA((parts,)),
        ],
        flops=2 * all_tokens * width * experts,
        nbytes=2 * all_tokens * width,
        name="score",
    )
    near = lax.all_to_all(products, ("y", "c"), 0, 0, tiled=True)
    far = call(
        functools.partial(near_kernel, along=along, rows=rows),
        jax.ShapeDtypeStruct((along, rows, experts), BF16),
        near,
        name="near",
    )
    far = lax.all_to_all(far, "z", 0, 0, tiled=True)

    chunk = 256 if width % 256 == 0 else width
    hidden_grad = call(
        functools.partial(hidden_kernel, rows=rows),
        jax.ShapeDtypeStruct((all_tokens, width), BF16),
        lax.axis_index("c").astype(jnp.int32)[None],
        score,
        across_parts,
        other_router,
        far=(0,),
        grid=(width // chunk,),
        in_specs=[
            pl.BlockSpec(memory_space=pltpu.SMEM),
            vmem,
            vmem,
            vmem,
        ],
        out_specs=pl.BlockSpec((all_tokens, chunk), lambda i: (0, i)),
        scratch_shapes=[pltpu.VMEM((width, experts), BF16)],
        flops=2 * all_tokens * width * experts,
        nbytes=2 * all_tokens * width,
        name="hidden_grad",
    )
    weight_grad = call(
        far_kernel, jax.ShapeDtypeStruct((rows, experts), F32), far, name="weight_grad"
    )
    return weight_grad, hidden_grad


def solution(mesh):
    dp, mp = mesh.devices.shape
    along = dp // 8
    split = Mesh(mesh.devices.reshape(4, along, 2, mp), ("y", "z", "c", "x"))
    token_rows = ("y", "z", "c", "x")
    weight_rows = ("x", "y", "z", "c")
    return jax.shard_map(
        body,
        mesh=split,
        in_specs=(
            P(DP, "x"),
            P(weight_rows, None),
            P(token_rows, None),
            P(),
            P(),
            P(token_rows),
            P(token_rows),
        ),
        out_specs=(P(weight_rows, None), P(DP, "x")),
        check_vma=False,
    )
```

time: 146 us -> 129 us (0.88)
  the two profiles are of different devices: /device:TPU:32 before, /device:TPU:2 now
where the time goes in v2:
time: 129 us
  waiting for transfers between devices  45.6 us (35%)
  starting transfers between devices  30.7 us (24%)
  blocking collectives  30.3 us (23%)
  Pallas kernels  19.7 us (15%)
  local copies, waits for them, and re-layouts  1.53 us (1%)
    pallas_call x12, Pallas kernels, call(): pl.pallas_call(kernel, out_shape=shapes, cost_estimate=pl.CostEstimate(fl...  19.7 us
    all_gather x1, blocking collectives, body(): gathered = lax.all_gather(exponents, 'x')  15.2 us
    all_gather x1, blocking collectives, body(): across_parts = lax.all_gather(sent, 'y')  13.3 us
    all_to_all x1, starting transfers between devices, body(): along_parts = lax.all_to_all(sent, 'z', 0, 0, tiled=True)  13 us
    all_to_all x1, waiting for transfers between devices, body(): along_parts = lax.all_to_all(sent, 'z', 0, 0, tiled=True)  12.8 us
    all_to_all x1, waiting for transfers between devices, body(): near = lax.all_to_all(products, ('y', 'c'), 0, 0, tiled=True)  12.1 us
    all_to_all x1, waiting for transfers between devices, body(): first_col = lax.all_to_all(partial_col, DP, 0, 0, tiled=True)  11.2 us
    all_to_all x1, waiting for transfers between devices, body(): far = lax.all_to_all(far, 'z', 0, 0, tiled=True)  9.55 us
  transfers between devices with their start and end apart: 5, of which 4 were waited for; matrix products, arithmetic and copies ran while one was open for 0% of the time, Pallas kernels for 9%

profile of v2, /device:TPU:2, one launch (start us, length us, event | category | flops | bytes accessed | tf_op | source)
XLA Modules:
  0.0 128.6 jit_solution(1190332482134871603)
XLA Ops:
  0.6 1.1 exponents.1
  1.7 15.2 %all-gather = bf16[768,256]{1,0:T(8,128)(2,1)S(1)} all-gather(bf16[192,256]{1,0:T(8,128)(2,1)S(1)} %get-tuple-element.12), channel_id=2, replica_groups=mesh['y'=4,'z'=16,'c'=2,'x'=4] {'x'}, dimensions={0}, use_global_device_ids=true | all-gather | bytes 491520 | tf_op jit(solution)/shard_map/all_gather | solution.py:276
  16.9 1.0 direct.1
  17.9 13.0 %all-to-all-start = ((bf16[16,16,256]{2,1,0:T(8,128)(2,1)}), bf16[16,16,256]{2,1,0:T(8,128)(2,1)S(1)}, u32[]{:S(2)}, u32[]{:S(2)}) async-start(bf16[16,16,256]{2,1,0:T(8,128)(2,1)} %direct.1), calls=%async_computation | async-start | bytes 262144 | tf_op jit(solution)/shard_map/all_to_all | solution.py:300
  30.9 0.4 prepared.1
  31.2 12.8 %all-to-all-done.parts_ref = bf16[16,16,256]{2,1,0:T(8,128)(2,1)S(1)} async-done(((bf16[16,16,256]{2,1,0:T(8,128)(2,1)}), bf16[16,16,256]{2,1,0:T(8,128)(2,1)S(1)}, u32[]{:S(2)}, u32[]{:S(2)}) %all-to-all-start) | async-done | bytes 131104 | tf_op jit(solution)/shard_map/all_to_all | solution.py:300
  44.1 13.3 %all-gather.1 = bf16[1024,256]{1,0:T(8,128)(2,1)S(1)} all-gather(bf16[256,256]{1,0:T(8,128)(2,1)S(1)} %along.1), channel_id=3, replica_groups=mesh['y'=4,'z'=16,'c'=2,'x'=4] {'y'}, dimensions={0}, use_global_device_ids=true | all-gather | bytes 655360 | tf_op jit(solution)/shard_map/all_gather | solution.py:316
  57.4 1.8 %all-gather.3.sums_ref = f32[2,1,256]{2,1,0:T(1,128)S(1)} all-gather(f32[1,1,256]{2,1,0:T(1,128)S(1)} %bitcast.14), channel_id=4, replica_groups=mesh['y'=4,'z'=16,'c'=2,'x'=4] {'c'}, dimensions={0}, use_global_device_ids=true | all-gather | bytes 3072 | tf_op jit(solution)/shard_map/all_gather | solution.py:323
  59.2 0.9 first_col.1
  60.1 8.3 %all-to-all-start.1 = ((f32[128,1,256]{2,1,0:T(1,128)}), f32[128,1,256]{2,1,0:T(1,128)S(1)}, u32[]{:S(2)}, u32[]{:S(2)}) async-start(f32[128,1,256]{2,1,0:T(1,128)} %first_col.1), calls=%async_computation.1 | async-start | bytes 262144 | tf_op jit(solution)/shard_map/all_to_all | solution.py:335
  68.4 4.9 %transposed.1.hidden_ref = bf16[1792,704]{1,0:T(8,128)(2,1)S(1)} custom-call(bf16[704,1792]{1,0:T(8,128)(2,1)} %hidden_ref.1), custom_call_target="tpu_custom_call" | custom-call | flops 2260729856 | bytes 5046272 | tf_op jit(solution)/shard_map/transposed/pallas_call | solution.py:26
  73.3 0.0 copy-start
  73.3 1.5 %copy-done = bf16[1792,704]{1,0:T(8,128)(2,1)} copy-done((bf16[1792,704]{1,0:T(8,128)(2,1)}, bf16[1792,704]{1,0:T(8,128)(2,1)S(1)}, u32[]{:S(2)}) %copy-start) | copy-done | bytes 2523160
  74.8 0.7 second.1
  75.5 11.2 %all-to-all-done.1.first_col_ref = f32[128,1,256]{2,1,0:T(1,128)S(1)} async-done(((f32[128,1,256]{2,1,0:T(1,128)}), f32[128,1,256]{2,1,0:T(1,128)S(1)}, u32[]{:S(2)}, u32[]{:S(2)}) %all-to-all-start.1) | async-done | bytes 131104 | tf_op jit(solution)/shard_map/all_to_all | solution.py:335
  86.7 4.6 %score.1 = (bf16[704,256]{1,0:T(8,128)(2,1)S(1)}, bf16[8,224,256]{2,1,0:T(8,128)(2,1)}) custom-call(f32[704,256]{1,0:T(8,128)S(1)} %get-tuple-element.15.second_ref, f32[704,256]{1,0:T(8,128)S(1)} %get-tuple-element.16.first_ref, f32[2,256]{1,0:T(2,128)S(1)} %get-tuple-element.13.gains_ref, f32[128,1,256]{2,1,0:T(1,128)S(1)} %all-to-all-done.1.first_col_ref, ...), custom_call_target="tpu_custom_call" | custom-call | flops 645922816 | bytes 2523136 | tf_op jit(solution)/shard_map/score/pallas_call | solution.py:26
  91.3 3.6 %all-to-all-start.2 = ((bf16[8,224,256]{2,1,0:T(8,128)(2,1)}), bf16[8,224,256]{2,1,0:T(8,128)(2,1)S(1)}, u32[]{:S(2)}, u32[]{:S(2)}) async-start(bf16[8,224,256]{2,1,0:T(8,128)(2,1)} %get-tuple-element.20), calls=%async_computation.2 | async-start | bytes 1835008 | tf_op jit(solution)/shard_map/all_to_all | solution.py:370
  94.8 2.3 %collective-permute-start = (bf16[4,256,256]{2,1,0:T(8,128)(2,1)S(1)}, bf16[4,256,256]{2,1,0:T(8,128)(2,1)S(1)}, u32[]{:S(2)}, u32[]{:S(2)}) collective-permute-start(bf16[4,256,256]{2,1,0:T(8,128)(2,1)S(1)} %bitcast.12), channel_id=1, source_target_pairs={{0,4},{4,0},{1,5},{5,1},{2,6},{6,2},{3,7},{7,3},{8,12},{12,8},{9,1... | collective-permute-start | bytes 1572872 | tf_op jit(solution)/shard_map/ppermute | solution.py:324
  97.1 12.1 %all-to-all-done.2.parts_ref = bf16[8,224,256]{2,1,0:T(8,128)(2,1)S(1)} async-done(((bf16[8,224,256]{2,1,0:T(8,128)(2,1)}), bf16[8,224,256]{2,1,0:T(8,128)(2,1)S(1)}, u32[]{:S(2)}, u32[]{:S(2)}) %all-to-all-start.2) | async-done | bytes 917536 | tf_op jit(solution)/shard_map/all_to_all | solution.py:370
  109.3 0.8 near.1
  110.1 3.5 %all-to-all-start.3 = ((bf16[16,14,256]{2,1,0:T(8,128)(2,1)}), bf16[16,14,256]{2,1,0:T(8,128)(2,1)S(1)}, u32[]{:S(2)}, u32[]{:S(2)}) async-start(bf16[16,14,256]{2,1,0:T(8,128)(2,1)} %near.1), calls=%async_computation.3 | async-start | bytes 262144 | tf_op jit(solution)/shard_map/all_to_all | solution.py:377
  113.6 0.0 collective-permute-done.other_ref
  113.6 4.8 %hidden_grad.1 = bf16[704,1792]{1,0:T(8,128)(2,1)} custom-call(s32[1]{0:T(128)} %bitcast.7.core_ref, bf16[704,256]{1,0:T(8,128)(2,1)S(1)} %get-tuple-element.21.score_ref, bf16[4,256,256]{2,1,0:T(8,128)(2,1)S(1)} %bitcast.13, bf16[4,256,256]{2,1,0:T(8,128)(2,1)S(1)} %collective-permute-done.other_ref), custom_call_target="tpu_custom_call" | custom-call | flops 645922816 | bytes 2523136 | tf_op jit(solution)/shard_map/hidden_grad/pallas_call | solution.py:26
  118.4 9.5 %all-to-all-done.3.parts_ref = bf16[16,14,256]{2,1,0:T(8,128)(2,1)S(1)} async-done(((bf16[16,14,256]{2,1,0:T(8,128)(2,1)}), bf16[16,14,256]{2,1,0:T(8,128)(2,1)S(1)}, u32[]{:S(2)}, u32[]{:S(2)}) %all-to-all-start.3) | async-done | bytes 114720 | tf_op jit(solution)/shard_map/all_to_all | solution.py:377
  127.9 0.6 weight_grad.1
  (2 shorter events, 0.1 us)
Async XLA Ops:
  17.9 26.1 %all-to-all-start = ((bf16[16,16,256]{2,1,0:T(8,128)(2,1)}), bf16[16,16,256]{2,1,0:T(8,128)(2,1)S(1)}, u32[]{:S(2)}, u32[]{:S(2)}) async-start(bf16[16,16,256]{2,1,0:T(8,128)(2,1)} %direct.1), calls=%async_computation | async-start | bytes 262144 | tf_op jit(solution)/shard_map/all_to_all | solution.py:300
  60.1 26.6 %all-to-all-start.1 = ((f32[128,1,256]{2,1,0:T(1,128)}), f32[128,1,256]{2,1,0:T(1,128)S(1)}, u32[]{:S(2)}, u32[]{:S(2)}) async-start(f32[128,1,256]{2,1,0:T(1,128)} %first_col.1), calls=%async_computation.1 | async-start | bytes 262144 | tf_op jit(solution)/shard_map/all_to_all | solution.py:335
  73.3 1.5 %copy-start = (bf16[1792,704]{1,0:T(8,128)(2,1)}, bf16[1792,704]{1,0:T(8,128)(2,1)S(1)}, u32[]{:S(2)}) copy-start(bf16[1792,704]{1,0:T(8,128)(2,1)S(1)} %transposed.1.hidden_ref) | copy-start | bytes 7569412
  91.3 18.0 %all-to-all-start.2 = ((bf16[8,224,256]{2,1,0:T(8,128)(2,1)}), bf16[8,224,256]{2,1,0:T(8,128)(2,1)S(1)}, u32[]{:S(2)}, u32[]{:S(2)}) async-start(bf16[8,224,256]{2,1,0:T(8,128)(2,1)} %get-tuple-element.20), calls=%async_computation.2 | async-start | bytes 1835008 | tf_op jit(solution)/shard_map/all_to_all | solution.py:370
  94.8 18.8 %collective-permute-start = (bf16[4,256,256]{2,1,0:T(8,128)(2,1)S(1)}, bf16[4,256,256]{2,1,0:T(8,128)(2,1)S(1)}, u32[]{:S(2)}, u32[]{:S(2)}) collective-permute-start(bf16[4,256,256]{2,1,0:T(8,128)(2,1)S(1)} %bitcast.12), channel_id=1, source_target_pairs={{0,4},{4,0},{1,5},{5,1},{2,6},{6,2},{3,7},{7,3},{8,12},{12,8},{9,1... | collective-permute-start | bytes 1572872 | tf_op jit(solution)/shard_map/ppermute | solution.py:324
  110.1 17.9 %all-to-all-start.3 = ((bf16[16,14,256]{2,1,0:T(8,128)(2,1)}), bf16[16,14,256]{2,1,0:T(8,128)(2,1)S(1)}, u32[]{:S(2)}, u32[]{:S(2)}) async-start(bf16[16,14,256]{2,1,0:T(8,128)(2,1)} %near.1), calls=%async_computation.3 | async-start | bytes 262144 | tf_op jit(solution)/shard_map/all_to_all | solution.py:377

commit v3 on v2

--- a/solution.py
+++ b/solution.py
@@ -46,28 +46,39 @@
 
 
 def exponent_kernel(
-    logits_ref, index_ref, grad_ref, first_ref, second_ref, router_ref, out_ref, gains_ref, copy_ref
+    logits_ref, index_ref, grad_ref, first_ref, second_ref, router_ref, out_ref, gains_ref, sent_ref
 ):
     tokens, experts = logits_ref.shape
     logits = logits_ref[...]
     weight = jnp.exp(logits - jnp.max(logits, axis=1, keepdims=True))
     index = as_column(index_ref[...].astype(F32), tokens)
-    lane = lax.broadcasted_iota(jnp.int32, (tokens, experts), 1).astype(F32)
-    out_ref[:tokens, :] = jnp.where(lane == index, -weight, weight).astype(BF16)
+    hit = lax.broadcasted_iota(jnp.int32, (tokens, experts), 1).astype(F32) == index
+    signed = jnp.where(hit, -weight, weight).astype(BF16)
+    out_ref[:tokens, :] = signed
     high, low = split_two(grad_ref[...])
     rows = out_ref.shape[0] - tokens
     out_ref[tokens:, :] = jnp.zeros((rows, experts), BF16)
     row = lax.broadcasted_iota(jnp.int32, (rows, tokens), 0)
     tail = jnp.where(row == 0, high, jnp.where(row == 1, low, 0.0))
     out_ref[tokens:, :tokens] = tail.astype(BF16)
-    gains_ref[0:1, :] = jnp.exp(first_ref[...])
-    gains_ref[1:2, :] = jnp.exp(second_ref[...])
-    copy_ref[...] = router_ref[...]
-
-
-def tokens_of(gathered_ref, gains_ref, block, tokens):
-    signed = gathered_ref[block, :tokens, :].astype(F32)
-    tail = gathered_ref[block, tokens:, :].astype(F32)
+    first_gain = jnp.exp(first_ref[...])
+    second_gain = jnp.exp(second_ref[...])
+    gains_ref[0:1, :] = first_gain
+    gains_ref[1:2, :] = second_gain
+    weight = jnp.abs(signed.astype(F32))
+    scale = as_column(high + low, tokens) / jnp.sum(weight * first_gain, axis=1, keepdims=True)
+    total = jnp.sum(jnp.where(hit, weight * scale, 0.0), axis=0, keepdims=True)
+    high, low = split_two(total * second_gain)
+    rows = router_ref.shape[0]
+    for member in range(sent_ref.shape[0]):
+        sent_ref[member, :rows, :] = router_ref[...]
+        sent_ref[member, rows : rows + 1, :] = high.astype(BF16)
+        sent_ref[member, rows + 1 : rows + 2, :] = low.astype(BF16)
+
+
+def tokens_of(gathered_ref, gains_ref, tokens):
+    signed = gathered_ref[:tokens, :].astype(F32)
+    tail = gathered_ref[tokens:, :].astype(F32)
     grad = as_column(tail[0:1, :] + tail[1:2, :], tokens)
     weight = jnp.abs(signed)
     second_scale = 1.0 / jnp.sum(weight * gains_ref[0:1, :], axis=1, keepdims=True)
@@ -75,22 +86,10 @@
     return weight, second_scale, hot
 
 
-def direct_kernel(gathered_ref, gains_ref, router_ref, out_ref, *, tokens):
-    total = 0.0
-    for block in range(gathered_ref.shape[0]):
-        weight, second_scale, hot = tokens_of(gathered_ref, gains_ref, block, tokens)
-        total = total + jnp.sum(weight * hot * second_scale, axis=0, keepdims=True)
-    high, low = split_two(total * gains_ref[1:2, :])
-    rows = router_ref.shape[0]
-    for member in range(out_ref.shape[0]):
-        out_ref[member, :rows, :] = router_ref[...]
-        out_ref[member, rows : rows + 1, :] = high.astype(BF16)
-        out_ref[member, rows + 1 : rows + 2, :] = low.astype(BF16)
-
-
-def prepare_kernel(gathered_ref, gains_ref, direct_ref, prob_ref, soft_ref, *, tokens):
-    for block in range(gathered_ref.shape[0]):
-        weight, second_scale, hot = tokens_of(gathered_ref, gains_ref, block, tokens)
+def prepare_kernel(*refs, tokens, blocks):
+    gains_ref, direct_ref, prob_ref, soft_ref = refs[blocks:]
+    for block in range(blocks):
+        weight, second_scale, hot = tokens_of(refs[block], gains_ref, tokens)
         here = slice(block * tokens, (block + 1) * tokens)
         prob = weight * gains_ref[1:2, :] * second_scale
         prob_ref[here, :] = prob
@@ -99,24 +98,10 @@
 
 
 def along_kernel(parts_ref, out_ref, *, rows):
-    members = parts_ref.shape[0]
     pair = parts_ref[:, rows : rows + 2, :].astype(F32)
     total = jnp.sum(jnp.sum(pair, axis=0), axis=0, keepdims=True)
-    high, low = split_two(total)
-    for member in range(1, members):
-        out_ref[member * PAD : (member + 1) * PAD, :] = parts_ref[member]
-    block = parts_ref[0].astype(F32)
-    row = lax.broadcasted_iota(jnp.int32, block.shape, 0)
-    block = jnp.where(row == rows, high, jnp.where(row == rows + 1, low, block))
-    out_ref[0:PAD, :] = block.astype(BF16)
-
-
-def across_kernel(parts_ref, out_ref, *, rows):
-    total = 0.0
-    for member in range(parts_ref.shape[0]):
-        block = parts_ref[member, 0:PAD, :].astype(F32)
-        total = total + jnp.sum(block[rows : rows + 2, :], axis=0, keepdims=True)
-    out_ref[...] = total
+    for member in range(out_ref.shape[0]):
+        out_ref[member] = total
 
 
 def second_row_grad(direct, prob, scaled):
@@ -131,11 +116,13 @@
         out_ref[member] = total
 
 
-def second_kernel(gathered_ref, gains_ref, sums_ref, out_ref, first_ref, *, ratio, tokens):
+def second_kernel(place_ref, *refs, ratio, tokens, blocks):
+    gains_ref, sums_ref, out_ref, first_ref = refs[blocks:]
     scaled = ratio * jnp.sum(sums_ref[...], axis=0)
-    for block in range(gathered_ref.shape[0]):
-        weight, second_scale, hot = tokens_of(gathered_ref, gains_ref, block, tokens)
-        here = slice(block * tokens, (block + 1) * tokens)
+    for block in range(blocks):
+        weight, second_scale, hot = tokens_of(refs[block], gains_ref, tokens)
+        place = lax.rem(place_ref[0] + (blocks - block), blocks)
+        here = pl.ds(pl.multiple_of(place * tokens, tokens), tokens)
         left = weight * second_scale * (gains_ref[1:2, :] * (hot - scaled))
         row = jnp.sum(left, axis=1, keepdims=True)
         out_ref[here, :] = left - weight * gains_ref[0:1, :] * (second_scale * row)
@@ -217,7 +204,7 @@
     out_ref[...] = total
 
 
-def hidden_kernel(core_ref, score_ref, mine_ref, other_ref, out_ref, router_ref, *, rows):
+def hidden_kernel(place_ref, score_ref, mine_ref, other_ref, out_ref, router_ref, *, rows):
     members, padded, _ = mine_ref.shape
     along = padded // PAD
     size = 2 * along * rows
@@ -229,15 +216,17 @@
         place = whole_part(column, PAD)
         row = column - place * PAD
         base = place * (2 * rows) + row
-        kept = row < rows
-        mine_at = core_ref[0].astype(F32) * rows
-        mine = jnp.where(kept & (target == base + mine_at), 1.0, 0.0).astype(BF16)
-        other = jnp.where(kept & (target == base + (rows - mine_at)), 1.0, 0.0).astype(BF16)
+        kept_row = row < rows
+        mine_at = place_ref[0].astype(F32) * rows
+        mine = jnp.where(kept_row & (target == base + mine_at), 1.0, 0.0).astype(BF16)
+        other = jnp.where(kept_row & (target == base + (rows - mine_at)), 1.0, 0.0).astype(BF16)
         for member in range(members):
             whole = jnp.dot(mine, mine_ref[member], preferred_element_type=F32) + jnp.dot(
                 other, other_ref[member], preferred_element_type=F32
             )
-            router_ref[member * size : (member + 1) * size, :] = whole.astype(BF16)
+            at = lax.rem(place_ref[1] + (members - member), members)
+            start = pl.multiple_of(at * size, size)
+            router_ref[pl.ds(start, size), :] = whole.astype(BF16)
 
     width = out_ref.shape[1]
     start = pl.multiple_of(pl.program_id(0) * width, width)
@@ -249,6 +238,15 @@
     ).astype(BF16)
 
 
+def ahead(array, axis, step):
+    size = lax.axis_size(axis)
+    return lax.ppermute(array, axis, [(at, (at + step) % size) for at in range(size)])
+
+
+def index_of(axis):
+    return lax.axis_index(axis).astype(jnp.int32)
+
+
 def body(hidden, router_weight, logits, first_pot, second_pot, expert_index, loss_grad):
     tokens, experts = logits.shape
     rows = router_weight.shape[0]
@@ -257,12 +255,12 @@
     ratio = experts / (tokens * blocks * lax.axis_size(DP))
     all_tokens, width = hidden.shape
     vmem = pl.BlockSpec(memory_space=pltpu.VMEM)
-    exponents, gains, router = call(
+    exponents, gains, sent = call(
         exponent_kernel,
         (
             kept((tokens + PAD, experts), BF16),
             kept((2, experts), F32),
-            kept((rows, experts), BF16),
+            jax.ShapeDtypeStruct((along, PAD, experts), BF16),
         ),
         logits,
         expert_index[None],
@@ -273,7 +271,8 @@
         far=range(6),
         name="exponents",
     )
-    gathered = lax.all_gather(exponents, "x")
+    along_parts = lax.all_to_all(sent, "z", 0, 0, tiled=True)
+    gathered = [exponents] + [ahead(exponents, "x", step) for step in range(1, blocks)]
     whole = (all_tokens, experts)
 
     transposed = call(
@@ -289,19 +288,10 @@
         name="transposed",
     )
 
-    sent = call(
-        functools.partial(direct_kernel, tokens=tokens),
-        jax.ShapeDtypeStruct((along, PAD, experts), BF16),
-        gathered,
-        gains,
-        router,
-        name="direct",
-    )
-    along_parts = lax.all_to_all(sent, "z", 0, 0, tiled=True)
     direct, prob, soft = call(
-        functools.partial(prepare_kernel, tokens=tokens),
+        functools.partial(prepare_kernel, tokens=tokens, blocks=blocks),
         (kept(whole, F32),) * 3,
-        gathered,
+        *gathered,
         gains,
         flops=40 * all_tokens * experts,
         nbytes=14 * all_tokens * experts,
@@ -309,19 +299,13 @@
     )
     sent = call(
         functools.partial(along_kernel, rows=rows),
-        kept((along * PAD, experts), BF16),
+        jax.ShapeDtypeStruct((2 * across * blocks, 1, experts), F32),
         along_parts,
         name="along",
     )
-    across_parts = lax.all_gather(sent, "y")
-    sent = call(
-        functools.partial(across_kernel, rows=rows),
-        kept((1, experts), F32),
-        across_parts,
-        name="across",
-    )
-    sums = lax.all_gather(sent, "c")
-    other_router = lax.ppermute(across_parts, "c", [(0, 1), (1, 0)])
+    sums = lax.all_to_all(sent, ("c", "y", "x"), 0, 0, tiled=True)
+    mine = along_parts.reshape(1, along * PAD, experts)
+    mine = jnp.concatenate([mine] + [ahead(mine, "y", step) for step in range(1, across)])
 
     partial_col = call(
         functools.partial(first_col_kernel, ratio=ratio),
@@ -334,16 +318,21 @@
     )
     first_col = lax.all_to_all(partial_col, DP, 0, 0, tiled=True)
     second, first = call(
-        functools.partial(second_kernel, ratio=ratio, tokens=tokens),
+        functools.partial(second_kernel, ratio=ratio, tokens=tokens, blocks=blocks),
         (kept(whole, F32), kept(whole, F32)),
-        gathered,
+        index_of("x")[None],
+        *gathered,
         gains,
         sums,
         flops=40 * all_tokens * experts,
         nbytes=10 * all_tokens * experts,
+        in_specs=[pl.BlockSpec(memory_space=pltpu.SMEM)] + [vmem] * (blocks + 2),
+        far=(0,),
         name="second",
     )
 
+    second, mine = lax.optimization_barrier((second, mine))
+    other = ahead(mine, "c", 1)
     parts = 2 * across
     score, products = call(
         functools.partial(score_kernel, ratio=ratio),
@@ -380,10 +369,10 @@
     hidden_grad = call(
         functools.partial(hidden_kernel, rows=rows),
         jax.ShapeDtypeStruct((all_tokens, width), BF16),
-        lax.axis_index("c").astype(jnp.int32)[None],
+        jnp.stack([index_of("c"), index_of("y")]),
         score,
-        across_parts,
-        other_router,
+        mine,
+        other,
         far=(0,),
         grid=(width // chunk,),
         in_specs=[

time: 129 us -> 127 us (0.984)
  the two profiles are of different devices: /device:TPU:2 before, /device:TPU:32 now
where the time goes in v3:
time: 127 us; the launch traced here: 126 us
  starting transfers between devices  72.4 us (57%)
  waiting for transfers between devices  29.8 us (23%)
  Pallas kernels  20.8 us (16%)
  local copies, waits for them, and re-layouts  1.55 us (1%)
    ppermute x7, starting transfers between devices, ahead(): lax.ppermute(array, axis, [(at, (at + step) % size) for at in range(size)])  25.3 us
    pallas_call x10, Pallas kernels, call(): pl.pallas_call(kernel, out_shape=shapes, cost_estimate=pl.CostEstimate(fl...  20.8 us
    all_to_all x1, starting transfers between devices, body(): along_parts = lax.all_to_all(sent, 'z', 0, 0, tiled=True)  15.2 us
    all_to_all x1, waiting for transfers between devices, body(): near = lax.all_to_all(products, ('y', 'c'), 0, 0, tiled=True)  12.1 us
    all_to_all x1, starting transfers between devices, body(): far = lax.all_to_all(far, 'z', 0, 0, tiled=True)  12.1 us
    all_to_all x1, starting transfers between devices, body(): first_col = lax.all_to_all(partial_col, DP, 0, 0, tiled=True)  8.81 us
    all_to_all x1, waiting for transfers between devices, body(): far = lax.all_to_all(far, 'z', 0, 0, tiled=True)  7.78 us
    all_to_all x1, starting transfers between devices, body(): sums = lax.all_to_all(sent, ('c', 'y', 'x'), 0, 0, tiled=True)  7.32 us
  transfers between devices with their start and end apart: 12, of which 4 were waited for; matrix products, arithmetic and copies ran while one was open for 1% of the time, Pallas kernels for 10%

profile of v3, /device:TPU:32, one launch (start us, length us, event | category | flops | bytes accessed | tf_op | source)
XLA Modules:
  0.0 126.0 jit_solution(12582518039690588990)
XLA Ops:
  0.6 1.9 %exponents.1 = (bf16[192,256]{1,0:T(8,128)(2,1)S(1)}, f32[2,256]{1,0:T(2,128)S(1)}, bf16[16,16,256]{2,1,0:T(8,128)(2,1)}) custom-call(f32[176,256]{1,0:T(8,128)} %logits_ref.1, s32[1,176]{1,0:T(1,128)} %bitcast.12, f32[1,176]{1,0:T(1,128)} %bitcast.13, f32[1,256]{1,0:T(1,128)} %bitcast.14, f32[1,256]{1,0:T(1,128)} %bitcast.15, bf16[14,256]{1,0:T(8,128)(2,1)} %router_ref.1), custom_call_target="tpu_custom_call" | custom-call | tf_op jit(solution)/shard_map/exponents/pallas_call | solution.py:26
  2.5 15.2 %all-to-all-start = ((bf16[16,16,256]{2,1,0:T(8,128)(2,1)}), bf16[16,16,256]{2,1,0:T(8,128)(2,1)S(1)}, u32[]{:S(2)}, u32[]{:S(2)}) async-start(bf16[16,16,256]{2,1,0:T(8,128)(2,1)} %get-tuple-element.16), calls=%async_computation | async-start | bytes 262144 | tf_op jit(solution)/shard_map/all_to_all | solution.py:274
  17.7 3.4 %collective-permute-start = (bf16[192,256]{1,0:T(8,128)(2,1)S(1)}, bf16[192,256]{1,0:T(8,128)(2,1)S(1)}, u32[]{:S(2)}, u32[]{:S(2)}) collective-permute-start(bf16[192,256]{1,0:T(8,128)(2,1)S(1)} %get-tuple-element.14.refs_0_), channel_id=1, source_target_pairs={{0,1},{1,2},{2,3},{3,0},{4,5},{5,6},{6,7},{7,4},{8,9},{9,10},{10,1... | collective-permute-start | bytes 294920 | tf_op jit(solution)/shard_map/ppermute | solution.py:243
  21.1 4.6 %collective-permute-start.1 = (bf16[192,256]{1,0:T(8,128)(2,1)S(1)}, bf16[192,256]{1,0:T(8,128)(2,1)S(1)}, u32[]{:S(2)}, u32[]{:S(2)}) collective-permute-start(bf16[192,256]{1,0:T(8,128)(2,1)S(1)} %get-tuple-element.14.refs_0_), channel_id=1, source_target_pairs={{0,2},{1,3},{2,0},{3,1},{4,6},{5,7},{6,4},{7,5},{8,10},{9,11},{10,... | collective-permute-start | bytes 294920 | tf_op jit(solution)/shard_map/ppermute | solution.py:243
  25.8 3.3 %collective-permute-start.2 = (bf16[192,256]{1,0:T(8,128)(2,1)S(1)}, bf16[192,256]{1,0:T(8,128)(2,1)S(1)}, u32[]{:S(2)}, u32[]{:S(2)}) collective-permute-start(bf16[192,256]{1,0:T(8,128)(2,1)S(1)} %get-tuple-element.14.refs_0_), channel_id=1, source_target_pairs={{0,3},{1,0},{2,1},{3,2},{4,7},{5,4},{6,5},{7,6},{8,11},{9,8},{10,9... | collective-permute-start | bytes 294920 | tf_op jit(solution)/shard_map/ppermute | solution.py:243
  29.1 2.8 %all-to-all-done.parts_ref = bf16[16,16,256]{2,1,0:T(8,128)(2,1)S(1)} async-done(((bf16[16,16,256]{2,1,0:T(8,128)(2,1)}), bf16[16,16,256]{2,1,0:T(8,128)(2,1)S(1)}, u32[]{:S(2)}, u32[]{:S(2)}) %all-to-all-start) | async-done | bytes 131104 | tf_op jit(solution)/shard_map/all_to_all | solution.py:274
  31.9 0.7 along.1
  32.6 7.3 %all-to-all-start.1 = ((f32[32,1,256]{2,1,0:T(1,128)}), f32[32,1,256]{2,1,0:T(1,128)S(1)}, u32[]{:S(2)}, u32[]{:S(2)}) async-start(f32[32,1,256]{2,1,0:T(1,128)} %along.1), calls=%async_computation.1 | async-start | bytes 65536 | tf_op jit(solution)/shard_map/all_to_all | solution.py:306
  39.9 0.0 collective-permute-done.1.refs_2_
  40.0 0.0 collective-permute-done.2.refs_3_
  40.0 0.4 prepared.1
  40.3 7.0 %all-to-all-done.1.refs_5_.sums_ref = f32[32,1,256]{2,1,0:T(1,128)S(1)} async-done(((f32[32,1,256]{2,1,0:T(1,128)}), f32[32,1,256]{2,1,0:T(1,128)S(1)}, u32[]{:S(2)}, u32[]{:S(2)}) %all-to-all-start.1) | async-done | bytes 32800 | tf_op jit(solution)/shard_map/all_to_all | solution.py:306
  47.3 0.9 first_col.1
  48.2 8.8 %all-to-all-start.2 = ((f32[128,1,256]{2,1,0:T(1,128)}), f32[128,1,256]{2,1,0:T(1,128)S(1)}, u32[]{:S(2)}, u32[]{:S(2)}) async-start(f32[128,1,256]{2,1,0:T(1,128)} %first_col.1), calls=%async_computation.2 | async-start | bytes 262144 | tf_op jit(solution)/shard_map/all_to_all | solution.py:319
  57.1 3.5 %collective-permute-start.3 = (bf16[1,256,256]{2,1,0:T(8,128)(2,1)S(1)}, bf16[1,256,256]{2,1,0:T(8,128)(2,1)S(1)}, u32[]{:S(2)}, u32[]{:S(2)}) collective-permute-start(bf16[1,256,256]{2,1,0:T(8,128)(2,1)S(1)} %bitcast.8), channel_id=1, source_target_pairs={{0,128},{128,256},{256,384},{384,0},{1,129},{129,257},{257,385},{3... | collective-permute-start | bytes 393224 | tf_op jit(solution)/shard_map/ppermute | solution.py:243
  60.6 5.0 %collective-permute-start.4 = (bf16[1,256,256]{2,1,0:T(8,128)(2,1)S(1)}, bf16[1,256,256]{2,1,0:T(8,128)(2,1)S(1)}, u32[]{:S(2)}, u32[]{:S(2)}) collective-permute-start(bf16[1,256,256]{2,1,0:T(8,128)(2,1)S(1)} %bitcast.9), channel_id=1, source_target_pairs={{0,256},{128,384},{256,0},{384,128},{1,257},{129,385},{257,1},{385... | collective-permute-start | bytes 393224 | tf_op jit(solution)/shard_map/ppermute | solution.py:243
  65.6 3.2 %collective-permute-start.5 = (bf16[1,256,256]{2,1,0:T(8,128)(2,1)S(1)}, bf16[1,256,256]{2,1,0:T(8,128)(2,1)S(1)}, u32[]{:S(2)}, u32[]{:S(2)}) collective-permute-start(bf16[1,256,256]{2,1,0:T(8,128)(2,1)S(1)} %bitcast.10), channel_id=1, source_target_pairs={{0,384},{128,0},{256,128},{384,256},{1,385},{129,1},{257,129},{385... | collective-permute-start | bytes 393224 | tf_op jit(solution)/shard_map/ppermute | solution.py:243
  68.7 4.9 %transposed.1.hidden_ref = bf16[1792,704]{1,0:T(8,128)(2,1)S(1)} custom-call(bf16[704,1792]{1,0:T(8,128)(2,1)} %hidden_ref.1), custom_call_target="tpu_custom_call" | custom-call | flops 2260729856 | bytes 5046272 | tf_op jit(solution)/shard_map/transposed/pallas_call | solution.py:26
  73.6 1.6 %copy-done = bf16[1792,704]{1,0:T(8,128)(2,1)} copy-done((bf16[1792,704]{1,0:T(8,128)(2,1)}, bf16[1792,704]{1,0:T(8,128)(2,1)S(1)}, u32[]{:S(2)}) %copy-start) | copy-done | bytes 2523160
  75.2 0.7 second.1
  75.8 0.0 collective-permute-done.3
  75.9 0.1 pad_maximum_fusion.mine_ref
  76.0 4.6 %score.1 = (bf16[704,256]{1,0:T(8,128)(2,1)S(1)}, bf16[8,224,256]{2,1,0:T(8,128)(2,1)}) custom-call(f32[704,256]{1,0:T(8,128)S(1)} %get-tuple-element.18.second_ref, f32[704,256]{1,0:T(8,128)S(1)} %get-tuple-element.19.first_ref, f32[2,256]{1,0:T(2,128)S(1)} %get-tuple-element.15.refs_4_.gains_ref, f32[128,1,256]{2,1,0:T(1,128)S(1)} %all-to-all-done.2.first_col_ref, ...), custom_call_target="tpu_custom_call" | custom-call | flops 645922816 | bytes 2523136 | tf_op jit(solution)/shard_map/score/pallas_call | solution.py:26
  80.6 3.6 %all-to-all-start.3 = ((bf16[8,224,256]{2,1,0:T(8,128)(2,1)}), bf16[8,224,256]{2,1,0:T(8,128)(2,1)S(1)}, u32[]{:S(2)}, u32[]{:S(2)}) async-start(bf16[8,224,256]{2,1,0:T(8,128)(2,1)} %get-tuple-element.23), calls=%async_computation.3 | async-start | bytes 1835008 | tf_op jit(solution)/shard_map/all_to_all | solution.py:359
  84.1 2.3 %collective-permute-start.6 = (bf16[4,256,256]{2,1,0:T(8,128)(2,1)S(1)}, bf16[4,256,256]{2,1,0:T(8,128)(2,1)S(1)}, u32[]{:S(2)}, u32[]{:S(2)}) collective-permute-start(bf16[4,256,256]{2,1,0:T(8,128)(2,1)S(1)} %pad_maximum_fusion.mine_ref), channel_id=1, source_target_pairs={{0,4},{4,0},{1,5},{5,1},{2,6},{6,2},{3,7},{7,3},{8,12},{12,8},{9,1... | collective-permute-start | bytes 1572872 | tf_op jit(solution)/shard_map/ppermute | solution.py:243
  86.5 12.1 %all-to-all-done.3.parts_ref = bf16[8,224,256]{2,1,0:T(8,128)(2,1)S(1)} async-done(((bf16[8,224,256]{2,1,0:T(8,128)(2,1)}), bf16[8,224,256]{2,1,0:T(8,128)(2,1)S(1)}, u32[]{:S(2)}, u32[]{:S(2)}) %all-to-all-start.3) | async-done | bytes 917536 | tf_op jit(solution)/shard_map/all_to_all | solution.py:359
  98.6 0.8 near.1
  99.4 12.1 %all-to-all-start.4 = ((bf16[16,14,256]{2,1,0:T(8,128)(2,1)}), bf16[16,14,256]{2,1,0:T(8,128)(2,1)S(1)}, u32[]{:S(2)}, u32[]{:S(2)}) async-start(bf16[16,14,256]{2,1,0:T(8,128)(2,1)} %near.1), calls=%async_computation.4 | async-start | bytes 262144 | tf_op jit(solution)/shard_map/all_to_all | solution.py:366
  111.5 0.6 pad_add_fusion.place_ref
  112.1 5.4 %hidden_grad.1 = bf16[704,1792]{1,0:T(8,128)(2,1)} custom-call(s32[2]{0:T(128)} %pad_add_fusion.place_ref, bf16[704,256]{1,0:T(8,128)(2,1)S(1)} %get-tuple-element.24.score_ref, bf16[4,256,256]{2,1,0:T(8,128)(2,1)S(1)} %pad_maximum_fusion.mine_ref, bf16[4,256,256]{2,1,0:T(8,128)(2,1)S(1)} %collective-permute-done.6.other_ref), custom_call_target="tpu_custom_call" | custom-call | flops 645922816 | bytes 2523136 | tf_op jit(solution)/shard_map/hidden_grad/pallas_call | solution.py:26
  117.6 7.8 %all-to-all-done.4.parts_ref = bf16[16,14,256]{2,1,0:T(8,128)(2,1)S(1)} async-done(((bf16[16,14,256]{2,1,0:T(8,128)(2,1)}), bf16[16,14,256]{2,1,0:T(8,128)(2,1)S(1)}, u32[]{:S(2)}, u32[]{:S(2)}) %all-to-all-start.4) | async-done | bytes 114720 | tf_op jit(solution)/shard_map/all_to_all | solution.py:366
  125.3 0.6 weight_grad.1
  (6 shorter events, 0.0 us)
Async XLA Ops:
  2.5 29.4 %all-to-all-start = ((bf16[16,16,256]{2,1,0:T(8,128)(2,1)}), bf16[16,16,256]{2,1,0:T(8,128)(2,1)S(1)}, u32[]{:S(2)}, u32[]{:S(2)}) async-start(bf16[16,16,256]{2,1,0:T(8,128)(2,1)} %get-tuple-element.16), calls=%async_computation | async-start | bytes 262144 | tf_op jit(solution)/shard_map/all_to_all | solution.py:274
  17.7 22.2 %collective-permute-start = (bf16[192,256]{1,0:T(8,128)(2,1)S(1)}, bf16[192,256]{1,0:T(8,128)(2,1)S(1)}, u32[]{:S(2)}, u32[]{:S(2)}) collective-permute-start(bf16[192,256]{1,0:T(8,128)(2,1)S(1)} %get-tuple-element.14.refs_0_), channel_id=1, source_target_pairs={{0,1},{1,2},{2,3},{3,0},{4,5},{5,6},{6,7},{7,4},{8,9},{9,10},{10,1... | collective-permute-start | bytes 294920 | tf_op jit(solution)/shard_map/ppermute | solution.py:243
  21.1 18.8 %collective-permute-start.1 = (bf16[192,256]{1,0:T(8,128)(2,1)S(1)}, bf16[192,256]{1,0:T(8,128)(2,1)S(1)}, u32[]{:S(2)}, u32[]{:S(2)}) collective-permute-start(bf16[192,256]{1,0:T(8,128)(2,1)S(1)} %get-tuple-element.14.refs_0_), channel_id=1, source_target_pairs={{0,2},{1,3},{2,0},{3,1},{4,6},{5,7},{6,4},{7,5},{8,10},{9,11},{10,... | collective-permute-start | bytes 294920 | tf_op jit(solution)/shard_map/ppermute | solution.py:243
  25.8 14.2 %collective-permute-start.2 = (bf16[192,256]{1,0:T(8,128)(2,1)S(1)}, bf16[192,256]{1,0:T(8,128)(2,1)S(1)}, u32[]{:S(2)}, u32[]{:S(2)}) collective-permute-start(bf16[192,256]{1,0:T(8,128)(2,1)S(1)} %get-tuple-element.14.refs_0_), channel_id=1, source_target_pairs={{0,3},{1,0},{2,1},{3,2},{4,7},{5,4},{6,5},{7,6},{8,11},{9,8},{10,9... | collective-permute-start | bytes 294920 | tf_op jit(solution)/shard_map/ppermute | solution.py:243
  32.6 14.7 %all-to-all-start.1 = ((f32[32,1,256]{2,1,0:T(1,128)}), f32[32,1,256]{2,1,0:T(1,128)S(1)}, u32[]{:S(2)}, u32[]{:S(2)}) async-start(f32[32,1,256]{2,1,0:T(1,128)} %along.1), calls=%async_computation.1 | async-start | bytes 65536 | tf_op jit(solution)/shard_map/all_to_all | solution.py:306
  48.2 27.7 %all-to-all-start.2 = ((f32[128,1,256]{2,1,0:T(1,128)}), f32[128,1,256]{2,1,0:T(1,128)S(1)}, u32[]{:S(2)}, u32[]{:S(2)}) async-start(f32[128,1,256]{2,1,0:T(1,128)} %first_col.1), calls=%async_computation.2 | async-start | bytes 262144 | tf_op jit(solution)/shard_map/all_to_all | solution.py:319
  57.1 18.8 %collective-permute-start.3 = (bf16[1,256,256]{2,1,0:T(8,128)(2,1)S(1)}, bf16[1,256,256]{2,1,0:T(8,128)(2,1)S(1)}, u32[]{:S(2)}, u32[]{:S(2)}) collective-permute-start(bf16[1,256,256]{2,1,0:T(8,128)(2,1)S(1)} %bitcast.8), channel_id=1, source_target_pairs={{0,128},{128,256},{256,384},{384,0},{1,129},{129,257},{257,385},{3... | collective-permute-start | bytes 393224 | tf_op jit(solution)/shard_map/ppermute | solution.py:243
  60.6 15.3 %collective-permute-start.4 = (bf16[1,256,256]{2,1,0:T(8,128)(2,1)S(1)}, bf16[1,256,256]{2,1,0:T(8,128)(2,1)S(1)}, u32[]{:S(2)}, u32[]{:S(2)}) collective-permute-start(bf16[1,256,256]{2,1,0:T(8,128)(2,1)S(1)} %bitcast.9), channel_id=1, source_target_pairs={{0,256},{128,384},{256,0},{384,128},{1,257},{129,385},{257,1},{385... | collective-permute-start | bytes 393224 | tf_op jit(solution)/shard_map/ppermute | solution.py:243
  65.6 10.3 %collective-permute-start.5 = (bf16[1,256,256]{2,1,0:T(8,128)(2,1)S(1)}, bf16[1,256,256]{2,1,0:T(8,128)(2,1)S(1)}, u32[]{:S(2)}, u32[]{:S(2)}) collective-permute-start(bf16[1,256,256]{2,1,0:T(8,128)(2,1)S(1)} %bitcast.10), channel_id=1, source_target_pairs={{0,384},{128,0},{256,128},{384,256},{1,385},{129,1},{257,129},{385... | collective-permute-start | bytes 393224 | tf_op jit(solution)/shard_map/ppermute | solution.py:243
  73.6 1.6 %copy-start = (bf16[1792,704]{1,0:T(8,128)(2,1)}, bf16[1792,704]{1,0:T(8,128)(2,1)S(1)}, u32[]{:S(2)}) copy-start(bf16[1792,704]{1,0:T(8,128)(2,1)S(1)} %transposed.1.hidden_ref) | copy-start | bytes 7569412
  80.6 18.0 %all-to-all-start.3 = ((bf16[8,224,256]{2,1,0:T(8,128)(2,1)}), bf16[8,224,256]{2,1,0:T(8,128)(2,1)S(1)}, u32[]{:S(2)}, u32[]{:S(2)}) async-start(bf16[8,224,256]{2,1,0:T(8,128)(2,1)} %get-tuple-element.23), calls=%async_computation.3 | async-start | bytes 1835008 | tf_op jit(solution)/shard_map/all_to_all | solution.py:359
  84.1 28.0 %collective-permute-start.6 = (bf16[4,256,256]{2,1,0:T(8,128)(2,1)S(1)}, bf16[4,256,256]{2,1,0:T(8,128)(2,1)S(1)}, u32[]{:S(2)}, u32[]{:S(2)}) collective-permute-start(bf16[4,256,256]{2,1,0:T(8,128)(2,1)S(1)} %pad_maximum_fusion.mine_ref), channel_id=1, source_target_pairs={{0,4},{4,0},{1,5},{5,1},{2,6},{6,2},{3,7},{7,3},{8,12},{12,8},{9,1... | collective-permute-start | bytes 1572872 | tf_op jit(solution)/shard_map/ppermute | solution.py:243
  99.4 26.0 %all-to-all-start.4 = ((bf16[16,14,256]{2,1,0:T(8,128)(2,1)}), bf16[16,14,256]{2,1,0:T(8,128)(2,1)S(1)}, u32[]{:S(2)}, u32[]{:S(2)}) async-start(bf16[16,14,256]{2,1,0:T(8,128)(2,1)} %near.1), calls=%async_computation.4 | async-start | bytes 262144 | tf_op jit(solution)/shard_map/all_to_all | solution.py:366

commit v4 on v3

v4 whole, which is shorter than its diff:
```python
import functools

import jax
import jax.numpy as jnp
from jax import lax
from jax.experimental import pallas as pl
from jax.experimental.pallas import tpu as pltpu
from jax.sharding import Mesh
from jax.sharding import PartitionSpec as P

DP = ("y", "z", "c")
F32 = jnp.float32
BF16 = jnp.bfloat16
PAD = 16


def kept(shape, dtype):
    return pltpu.VMEM(shape, dtype)


def outside(shape, dtype):
    return pltpu.HBM(shape, dtype)


def placed(array, near):
    return pltpu.with_memory_space_constraint(array, pltpu.VMEM if near else pltpu.HBM)


def call(kernel, shapes, *args, far=(), flops=0, nbytes=0, limit=16, **kwargs):
    return pl.pallas_call(
        kernel,
        out_shape=shapes,
        cost_estimate=pl.CostEstimate(flops=flops, transcendentals=0, bytes_accessed=nbytes),
        compiler_params=pltpu.CompilerParams(vmem_limit_bytes=limit << 20),
        **kwargs,
    )(*(placed(arg, at not in far) for at, arg in enumerate(args)))


def split_two(value):
    high = value.astype(BF16)
    low = (value - high.astype(F32)).astype(BF16)
    return high.astype(F32), low.astype(F32)


def as_column(row, tokens):
    shape = (tokens, row.shape[1])
    same = lax.broadcasted_iota(jnp.int32, shape, 0) == lax.broadcasted_iota(jnp.int32, shape, 1)
    return jnp.sum(jnp.where(same, row, 0.0), axis=1, keepdims=True)


def exponent_kernel(
    logits_ref, index_ref, grad_ref, first_ref, second_ref, router_ref, out_ref, gains_ref, sent_ref
):
    tokens, experts = logits_ref.shape
    logits = logits_ref[...]
    weight = jnp.exp(logits - jnp.max(logits, axis=1, keepdims=True))
    index = as_column(index_ref[...].astype(F32), tokens)
    hit = lax.broadcasted_iota(jnp.int32, (tokens, experts), 1).astype(F32) == index
    signed = jnp.where(hit, -weight, weight).astype(BF16)
    out_ref[:tokens, :] = signed
    high, low = split_two(grad_ref[...])
    rows = out_ref.shape[0] - tokens
    out_ref[tokens:, :] = jnp.zeros((rows, experts), BF16)
    row = lax.broadcasted_iota(jnp.int32, (rows, tokens), 0)
    tail = jnp.where(row == 0, high, jnp.where(row == 1, low, 0.0))
    out_ref[tokens:, :tokens] = tail.astype(BF16)
    first_gain = jnp.exp(first_ref[...])
    second_gain = jnp.exp(second_ref[...])
    gains_ref[0:1, :] = first_gain
    gains_ref[1:2, :] = second_gain
    weight = jnp.abs(signed.astype(F32))
    scale = as_column(high + low, tokens) / jnp.sum(weight * first_gain, axis=1, keepdims=True)
    total = jnp.sum(jnp.where(hit, weight * scale, 0.0), axis=0, keepdims=True)
    high, low = split_two(total * second_gain)
    rows = router_ref.shape[0]
    for member in range(sent_ref.shape[0]):
        sent_ref[member, :rows, :] = router_ref[...]
        sent_ref[member, rows : rows + 1, :] = high.astype(BF16)
        sent_ref[member, rows + 1 : rows + 2, :] = low.astype(BF16)


def tokens_of(gathered_ref, gains_ref, block, tokens):
    signed = gathered_ref[block, :tokens, :].astype(F32)
    tail = gathered_ref[block, tokens:, :].astype(F32)
    grad = as_column(tail[0:1, :] + tail[1:2, :], tokens)
    weight = jnp.abs(signed)
    second_scale = 1.0 / jnp.sum(weight * gains_ref[0:1, :], axis=1, keepdims=True)
    hot = jnp.where(signed < 0.0, grad, 0.0)
    return weight, second_scale, hot


def along_kernel(parts_ref, out_ref, *, rows):
    pair = parts_ref[:, rows : rows + 2, :].astype(F32)
    total = jnp.sum(jnp.sum(pair, axis=0), axis=0, keepdims=True)
    high, low = split_two(total)
    block = parts_ref[0].astype(F32)
    row = lax.broadcasted_iota(jnp.int32, block.shape, 0)
    block = jnp.where(row == rows, high, jnp.where(row == rows + 1, low, block)).astype(BF16)
    for copy in range(out_ref.shape[0]):
        out_ref[copy, 0:PAD, :] = block
        for member in range(1, parts_ref.shape[0]):
            out_ref[copy, member * PAD : (member + 1) * PAD, :] = parts_ref[member]


def across_kernel(parts_ref, exponents_ref, out_ref, *, rows, tokens):
    total = 0.0
    for member in range(parts_ref.shape[0]):
        block = parts_ref[member, 0:PAD, :].astype(F32)
        total = total + jnp.sum(block[rows : rows + 2, :], axis=0, keepdims=True)
    high, low = split_two(total)
    tail = exponents_ref[tokens:, :].astype(F32)
    row = lax.broadcasted_iota(jnp.int32, tail.shape, 0)
    tail = jnp.where(row == 2, high, jnp.where(row == 3, low, tail)).astype(BF16)
    for copy in range(out_ref.shape[0]):
        out_ref[copy, :tokens, :] = exponents_ref[:tokens, :]
        out_ref[copy, tokens:, :] = tail


def column_sum(gathered_ref, tokens):
    total = 0.0
    for block in range(gathered_ref.shape[0]):
        tail = gathered_ref[block, tokens:, :].astype(F32)
        total = total + jnp.sum(tail[2:4, :], axis=0, keepdims=True)
    return total


def first_col_kernel(gathered_ref, gains_ref, out_ref, *, ratio, tokens):
    scaled = ratio * column_sum(gathered_ref, tokens)
    total = 0.0
    for block in range(gathered_ref.shape[0]):
        weight, second_scale, hot = tokens_of(gathered_ref, gains_ref, block, tokens)
        left = weight * (gains_ref[1:2, :] * (hot - scaled))
        row = jnp.sum(left, axis=1, keepdims=True)
        total = total - jnp.sum(
            weight * (row * second_scale * second_scale), axis=0, keepdims=True
        )
    total = total * gains_ref[0:1, :]
    for member in range(out_ref.shape[0]):
        out_ref[member] = total


def sum_kernel(parts_ref, out_ref):
    total = jnp.sum(parts_ref[...], axis=0)
    for copy in range(out_ref.shape[0]):
        out_ref[copy] = total


def score_kernel(
    core_ref,
    gathered_ref,
    gains_ref,
    first_col_ref,
    mine_ref,
    other_ref,
    score_ref,
    out_ref,
    near_ref,
    half_ref,
    made_ref,
    half_done_ref,
    score_sent_ref,
    sent_ref,
    *,
    ratio,
    tokens,
):
    half_copy = pltpu.make_async_copy(other_ref, half_ref, half_done_ref)
    half_copy.start()
    scaled = ratio * column_sum(gathered_ref, tokens)
    first_scaled = ratio * gains_ref[0:1, :] * jnp.sum(first_col_ref[...], axis=0)
    blocks = gathered_ref.shape[0] // 2
    for side in range(2):
        start = (core_ref[0] * (1 - side) + (1 - core_ref[0]) * side) * blocks
        for block in range(blocks):
            weight, second_scale, hot = tokens_of(gathered_ref, gains_ref, start + block, tokens)
            left = second_scale * (gains_ref[1:2, :] * (hot - scaled))
            row = jnp.sum(weight * left, axis=1, keepdims=True)
            left = left - gains_ref[0:1, :] * (second_scale * row)
            first_scale = 1.0 / jnp.sum(weight, axis=1, keepdims=True)
            row = jnp.sum(weight * first_scaled, axis=1, keepdims=True) * first_scale
            score = weight * (left - first_scale * (first_scaled - row))
            near_ref[side, block * tokens : (block + 1) * tokens, :] = score.astype(BF16)
    score_copy = pltpu.make_async_copy(near_ref.at[0], score_ref, score_sent_ref)
    score_copy.start()
    half_copy.wait()
    parts = made_ref.shape[0]
    copies = []
    for part in range(parts):
        made_ref[part] = (
            jnp.dot(mine_ref[part], near_ref[0], preferred_element_type=F32)
            + jnp.dot(half_ref[part], near_ref[1], preferred_element_type=F32)
        ).astype(BF16)
        copies.append(
            pltpu.make_async_copy(made_ref.at[part], out_ref.at[part], sent_ref.at[part])
        )
        copies[part].start()
    score_copy.wait()
    for part in range(parts):
        copies[part].wait()


def whole_part(value, size):
    return jnp.floor((value + 0.5) * (1.0 / size))


def transpose_kernel(core_ref, hidden_ref, mine_ref, other_ref, *, along, rows):
    span = along * rows
    whole = hidden_ref.shape[1]
    mine = core_ref[0].astype(F32)
    orders = {}
    for member in range(whole // (2 * span)):
        start = member * 2 * span
        first = start // 128 * 128
        last = min(-(-(start + 2 * span) // 128) * 128, whole)
        key = (start - first, last - first)
        if key not in orders:
            target = lax.broadcasted_iota(jnp.int32, (2 * span, 128), 0).astype(F32)[:, 0:1]
            side = whole_part(target, span)
            core = mine + side * (1.0 - 2.0 * mine)
            rest = target - side * span
            place = whole_part(rest, rows)
            wanted = place * (2 * rows) + core * rows + (rest - place * rows) + key[0]
            source = lax.broadcasted_iota(jnp.int32, (2 * span, key[1]), 1).astype(F32)
            orders[key] = jnp.where(source == wanted, 1.0, 0.0).astype(BF16)
        both = lax.dot_general(
            orders[key],
            hidden_ref[:, first:last],
            (((1,), (1,)), ((), ())),
            preferred_element_type=F32,
        ).astype(BF16)
        mine_ref[member] = both[:span]
        other_ref[member] = both[span:]


def near_kernel(parts_ref, out_ref, *, along, rows):
    total = 0.0
    for member in range(parts_ref.shape[0]):
        total = total + parts_ref[member].astype(F32)
    for place in range(along):
        out_ref[place] = total[place * rows : (place + 1) * rows, :].astype(BF16)


def far_kernel(parts_ref, out_ref):
    total = 0.0
    for member in range(parts_ref.shape[0]):
        total = total + parts_ref[member].astype(F32)
    out_ref[...] = total


def hidden_kernel(place_ref, score_ref, mine_ref, other_ref, out_ref, router_ref, *, rows):
    members, padded, _ = mine_ref.shape
    along = padded // PAD
    size = 2 * along * rows

    @pl.when(pl.program_id(0) == 0)
    def _():
        target = lax.broadcasted_iota(jnp.int32, (size, padded), 0).astype(F32)
        column = lax.broadcasted_iota(jnp.int32, (size, padded), 1).astype(F32)
        place = whole_part(column, PAD)
        row = column - place * PAD
        base = place * (2 * rows) + row
        kept_row = row < rows
        mine_at = place_ref[0].astype(F32) * rows
        mine = jnp.where(kept_row & (target == base + mine_at), 1.0, 0.0).astype(BF16)
        other = jnp.where(kept_row & (target == base + (rows - mine_at)), 1.0, 0.0).astype(BF16)
        for member in range(members):
            whole = jnp.dot(mine, mine_ref[member], preferred_element_type=F32) + jnp.dot(
                other, other_ref[member], preferred_element_type=F32
            )
            router_ref[member * size : (member + 1) * size, :] = whole.astype(BF16)

    width = out_ref.shape[1]
    start = pl.multiple_of(pl.program_id(0) * width, width)
    out_ref[...] = lax.dot_general(
        score_ref[...],
        router_ref[pl.ds(start, width), :],
        (((1,), (1,)), ((), ())),
        preferred_element_type=F32,
    ).astype(BF16)


def ahead(array, axis, step):
    size = lax.axis_size(axis)
    return lax.ppermute(array, axis, [(at, (at + step) % size) for at in range(size)])


def index_of(axis):
    return lax.axis_index(axis).astype(jnp.int32)


def body(hidden, router_weight, logits, first_pot, second_pot, expert_index, loss_grad):
    tokens, experts = logits.shape
    rows = router_weight.shape[0]
    across, along = lax.axis_size("y"), lax.axis_size("z")
    blocks = lax.axis_size("x")
    ratio = experts / (tokens * blocks * lax.axis_size(DP))
    all_tokens, width = hidden.shape
    vmem = pl.BlockSpec(memory_space=pltpu.VMEM)
    exponents, gains, sent = call(
        exponent_kernel,
        (
            kept((tokens + PAD, experts), BF16),
            kept((2, experts), F32),
            jax.ShapeDtypeStruct((along, PAD, experts), BF16),
        ),
        logits,
        expert_index[None],
        loss_grad[None],
        first_pot[None],
        second_pot[None],
        router_weight,
        far=range(6),
    )
    sent, core = lax.optimization_barrier((sent, index_of("c")[None]))
    along_parts = lax.all_to_all(sent, "z", 0, 0, tiled=True)
    along_parts, hidden = lax.optimization_barrier((along_parts, hidden))
    whole = (all_tokens, experts)

    half = (across, along * rows, all_tokens)
    smem = pl.BlockSpec(memory_space=pltpu.SMEM)
    transposed, other_half = call(
        functools.partial(transpose_kernel, along=along, rows=rows),
        (kept(half, BF16), outside(half, BF16)),
        core,
        hidden,
        far=(0, 1),
        in_specs=[smem, vmem],
        out_specs=(vmem, vmem),
        flops=width * width * all_tokens,
        nbytes=4 * width * all_tokens,
        limit=32,
    )
    other_half = ahead(other_half, "c", 1)
    sent = call(
        functools.partial(along_kernel, rows=rows),
        kept((across, along * PAD, experts), BF16),
        along_parts,
    )
    across_parts = lax.all_to_all(sent, "y", 0, 0, tiled=True)
    across_parts, transposed = lax.optimization_barrier((across_parts, transposed))
    sent = call(
        functools.partial(across_kernel, rows=rows, tokens=tokens),
        kept((blocks, tokens + PAD, experts), BF16),
        across_parts,
        exponents,
    )
    gathered = lax.all_to_all(sent, "x", 0, 0, tiled=True)
    gathered = lax.all_gather(gathered, "c", tiled=True)
    gathered, other_half = lax.optimization_barrier((gathered, other_half))
    partial_col = call(
        functools.partial(first_col_kernel, ratio=ratio, tokens=tokens),
        kept((along, 1, experts), F32),
        gathered,
        gains,
    )
    partial_col = call(
        sum_kernel,
        kept((across, 1, experts), F32),
        lax.all_to_all(partial_col, "z", 0, 0, tiled=True),
    )
    first_col = lax.all_to_all(partial_col, "y", 0, 0, tiled=True)

    made = (across, along * rows, experts)
    score, products = call(
        functools.partial(score_kernel, ratio=ratio, tokens=tokens),
        (outside(whole, BF16), outside(made, BF16)),
        core,
        gathered,
        gains,
        first_col,
        transposed,
        other_half,
        far=(0, 5),
        in_specs=[smem] + [vmem] * 4 + [pl.BlockSpec(memory_space=pl.ANY)],
        out_specs=(pl.BlockSpec(memory_space=pl.ANY),) * 2,
        scratch_shapes=[
            pltpu.VMEM((2, *whole), BF16),
            pltpu.VMEM(half, BF16),
            pltpu.VMEM(made, BF16),
            pltpu.SemaphoreType.DMA,
            pltpu.SemaphoreType.DMA,
            pltpu.SemaphoreType.DMA((across,)),
        ],
        flops=2 * all_tokens * width * experts,
        nbytes=2 * all_tokens * width,
    )
    score, mine = lax.optimization_barrier((score, across_parts))
    other = ahead(mine, "c", 1)
    near = lax.all_to_all(products, "y", 0, 0, tiled=True)
    far = call(
        functools.partial(near_kernel, along=along, rows=rows),
        jax.ShapeDtypeStruct((along, rows, experts), BF16),
        near,
    )
    chunk = 896 if width % 896 == 0 else width
    hidden_grad = call(
        functools.partial(hidden_kernel, rows=rows),
        jax.ShapeDtypeStruct((all_tokens, width), BF16),
        core,
        score,
        mine,
        other,
        far=(0, 1),
        grid=(width // chunk,),
        in_specs=[
            pl.BlockSpec(memory_space=pltpu.SMEM),
            vmem,
            vmem,
            vmem,
        ],
        out_specs=pl.BlockSpec((all_tokens, chunk), lambda i: (0, i)),
        scratch_shapes=[pltpu.VMEM((width, experts), BF16)],
        flops=2 * all_tokens * width * experts,
        nbytes=2 * all_tokens * width,
    )
    far, hidden_grad = lax.optimization_barrier((far, hidden_grad))
    far = lax.all_to_all(far, "z", 0, 0, tiled=True)
    weight_grad = call(far_kernel, jax.ShapeDtypeStruct((rows, experts), F32), far)
    return weight_grad, hidden_grad


def solution(mesh):
    dp, mp = mesh.devices.shape
    along = dp // 8
    split = Mesh(mesh.devices.reshape(4, along, 2, mp), ("y", "z", "c", "x"))
    token_rows = ("y", "z", "c", "x")
    weight_rows = ("x", "y", "z", "c")

    return jax.shard_map(
        body,
        mesh=split,
        in_specs=(
            P(DP, "x"),
            P(weight_rows, None),
            P(token_rows, None),
            P(),
            P(),
            P(token_rows),
            P(token_rows),
        ),
        out_specs=(P(weight_rows, None), P(DP, "x")),
        check_vma=False,
    )
```

time: 127 us -> 131 us (1.031)
  blocking collectives: 0 us -> 112 us
  starting transfers between devices: 72.4 us -> 3.83 us
  waiting for transfers between devices: 29.8 us -> 0.01 us
  Pallas kernels: 20.8 us -> 14.5 us
  local copies, waits for them, and re-layouts: 1.55 us -> 0.01 us
    all_to_all x0 -> x7, blocking collectives: none -> 109 us  [the longest x1 29.2 us: body(): along_parts = lax.all_to_all(sent, 'z', 0, 0, tiled=True)]
    all_to_all x5 -> x0, starting transfers between devices: 47 us -> none  [the longest x1 15.2 us: body(): along_parts = lax.all_to_all(sent, 'z', 0, 0, tiled=True)]
    all_to_all x5 -> x0, waiting for transfers between devices: 29.8 us -> none  [the longest x1 12.1 us: body(): near = lax.all_to_all(products, ('y', 'c'), 0, 0, tiled=True)]
    ppermute x7 -> x2, starting transfers between devices: 25.3 us -> 3.83 us  [ahead(): lax.ppermute(array, axis, [(at, (at + step) % size) for at in range(size)])]
    pallas_call x10, Pallas kernels: 20.8 us -> 14.5 us  [call(): pl.pallas_call(kernel, out_shape=shapes, cost_estimate=pl.CostEstimate(fl...]
    all_gather x0 -> x1, blocking collectives: none -> 2.36 us  [body(): gathered = lax.all_gather(gathered, 'c', tiled=True)]
    unnamed x2, local copies, waits for them, and re-layouts: 1.55 us -> 0.01 us
  transfers between devices with their start and end apart: 12 -> 2, of which waited for: 4 -> 0; matrix products, arithmetic and copies ran while one was open for 1% -> 0% of each run, Pallas kernels for 10% -> 0%
where the time goes in v4:
time: 131 us
  blocking collectives  112 us (85%)
  Pallas kernels  14.5 us (11%)
  starting transfers between devices  3.83 us (3%)
    all_to_all x1, blocking collectives, body(): along_parts = lax.all_to_all(sent, 'z', 0, 0, tiled=True)  29.2 us
    all_to_all x1, blocking collectives, body(): far = lax.all_to_all(far, 'z', 0, 0, tiled=True)  17.8 us
    all_to_all x1, blocking collectives, body(): lax.all_to_all(partial_col, 'z', 0, 0, tiled=True)  15.3 us
    pallas_call x10, Pallas kernels, call(): pl.pallas_call(kernel, out_shape=shapes, cost_estimate=pl.CostEstimate(fl...  14.5 us
    all_to_all x1, blocking collectives, body(): across_parts = lax.all_to_all(sent, 'y', 0, 0, tiled=True)  14.4 us
    all_to_all x1, blocking collectives, body(): near = lax.all_to_all(products, 'y', 0, 0, tiled=True)  13.2 us
    all_to_all x1, blocking collectives, body(): gathered = lax.all_to_all(sent, 'x', 0, 0, tiled=True)  11.7 us
    all_to_all x1, blocking collectives, body(): first_col = lax.all_to_all(partial_col, 'y', 0, 0, tiled=True)  7.63 us
  transfers between devices with their start and end apart: 2, of which 0 were waited for; matrix products, arithmetic and copies ran while one was open for 0% of the time, Pallas kernels for 0%

profile of v4, /device:TPU:32, one launch (start us, length us, event | category | flops | bytes accessed | tf_op | source)
XLA Modules:
  0.0 130.7 jit_solution(6854391036567128121)
XLA Ops:
  0.6 1.2 shard_map.86
  1.9 29.2 %all_to_all.35.parts_ref = bf16[16,16,256]{2,1,0:T(8,128)(2,1)S(1)} all-to-all(bf16[16,16,256]{2,1,0:T(8,128)(2,1)S(1)} %get-tuple-element.23), channel_id=1, replica_groups=mesh['y'=4,'z'=16,'c'=2,'x'=4] {'z'}, dimensions={0} | all-to-all | bytes 262144 | tf_op jit(solution)/shard_map/all_to_all | solution.py:315
  31.1 4.4 %shard_map.88 = (bf16[4,224,704]{2,1,0:T(8,128)(2,1)S(1)}, bf16[4,224,704]{2,1,0:T(8,128)(2,1)}) custom-call(s32[1]{0:T(128)} %bitcast.4.core_ref.place_ref, bf16[704,1792]{1,0:T(8,128)(2,1)} %hidden_ref), custom_call_target="tpu_custom_call" | custom-call | flops 2260729856 | bytes 5046272 | tf_op jit(solution)/shard_map/pallas_call | solution.py:30
  35.5 1.9 %collective-permute-start = (bf16[4,224,704]{2,1,0:T(8,128)(2,1)}, bf16[4,224,704]{2,1,0:T(8,128)(2,1)S(1)}, u32[]{:S(2)}, u32[]{:S(2)}) collective-permute-start(bf16[4,224,704]{2,1,0:T(8,128)(2,1)} %get-tuple-element.29), channel_id=1, source_target_pairs={{0,4},{4,0},{1,5},{5,1},{2,6},{6,2},{3,7},{7,3},{8,12},{12,8},{9,1... | collective-permute-start | bytes 3784712 | tf_op jit(solution)/shard_map/ppermute | solution.py:284
  37.4 0.1 shard_map.87
  37.5 14.4 %all_to_all.36.parts_ref.mine_ref = bf16[4,256,256]{2,1,0:T(8,128)(2,1)S(1)} all-to-all(bf16[4,256,256]{2,1,0:T(8,128)(2,1)S(1)} %shard_map.87), channel_id=1, replica_groups=mesh['y'=4,'z'=16,'c'=2,'x'=4] {'y'}, dimensions={0} | all-to-all | bytes 1048576 | tf_op jit(solution)/shard_map/all_to_all | solution.py:339
  51.9 11.7 %all_to_all.37 = bf16[4,192,256]{2,1,0:T(8,128)(2,1)S(1)} all-to-all(bf16[4,192,256]{2,1,0:T(8,128)(2,1)S(1)} %shard_map.89), channel_id=1, replica_groups=mesh['y'=4,'z'=16,'c'=2,'x'=4] {'x'}, dimensions={0} | all-to-all | bytes 786432 | tf_op jit(solution)/shard_map/all_to_all | solution.py:347
  63.6 2.4 %all_gather.3.gathered_ref = bf16[8,192,256]{2,1,0:T(8,128)(2,1)S(1)} all-gather(bf16[4,192,256]{2,1,0:T(8,128)(2,1)S(1)} %all_to_all.37), channel_id=1, replica_groups=mesh['y'=4,'z'=16,'c'=2,'x'=4] {'c'}, dimensions={0}, use_global_device_ids=true | all-gather | bytes 1179648 | tf_op jit(solution)/shard_map/all_gather | solution.py:348
  66.0 0.0 collective-permute-done.other_ref
  66.0 0.0 copy-start
  66.0 1.0 shard_map.90
  67.0 15.3 %all_to_all.38.parts_ref = f32[16,1,256]{2,1,0:T(1,128)S(1)} all-to-all(f32[16,1,256]{2,1,0:T(1,128)S(1)} %shard_map.90), channel_id=1, replica_groups=mesh['y'=4,'z'=16,'c'=2,'x'=4] {'z'}, dimensions={0} | all-to-all | bytes 32768 | tf_op jit(solution)/shard_map/all_to_all | solution.py:359
  82.3 7.6 %all_to_all.39.first_col_ref = f32[4,1,256]{2,1,0:T(1,128)S(1)} all-to-all(f32[4,1,256]{2,1,0:T(1,128)S(1)} %shard_map.91), channel_id=1, replica_groups=mesh['y'=4,'z'=16,'c'=2,'x'=4] {'y'}, dimensions={0} | all-to-all | bytes 8192 | tf_op jit(solution)/shard_map/all_to_all | solution.py:361
  90.0 0.0 copy-done
  90.0 3.2 %shard_map.92 = (bf16[704,256]{1,0:T(8,128)(2,1)}, bf16[4,224,256]{2,1,0:T(8,128)(2,1)}) custom-call(s32[1]{0:T(128)} %bitcast.4.core_ref.place_ref, bf16[8,192,256]{2,1,0:T(8,128)(2,1)S(1)} %all_gather.3.gathered_ref, f32[2,256]{1,0:T(2,128)S(1)} %get-tuple-element.31.gains_ref, f32[4,1,256]{2,1,0:T(1,128)S(1)} %all_to_all.39.first_col_ref, ...), custom_call_target="tpu_custom_call" | custom-call | flops 645922816 | bytes 2523136 | tf_op jit(solution)/shard_map/pallas_call | solution.py:30
  93.2 1.9 %collective-permute-start.1 = (bf16[4,256,256]{2,1,0:T(8,128)(2,1)S(1)}, bf16[4,256,256]{2,1,0:T(8,128)(2,1)S(1)}, u32[]{:S(2)}, u32[]{:S(2)}) collective-permute-start(bf16[4,256,256]{2,1,0:T(8,128)(2,1)S(1)} %all_to_all.36.parts_ref.mine_ref), channel_id=1, source_target_pairs={{0,4},{4,0},{1,5},{5,1},{2,6},{6,2},{3,7},{7,3},{8,12},{12,8},{9,1... | collective-permute-start | bytes 1572872 | tf_op jit(solution)/shard_map/ppermute | solution.py:284
  95.1 13.2 %all_to_all.40.parts_ref = bf16[4,224,256]{2,1,0:T(8,128)(2,1)S(1)} all-to-all(bf16[4,224,256]{2,1,0:T(8,128)(2,1)} %get-tuple-element.34), channel_id=1, replica_groups=mesh['y'=4,'z'=16,'c'=2,'x'=4] {'y'}, dimensions={0} | all-to-all | bytes 917504 | tf_op jit(solution)/shard_map/all_to_all | solution.py:389
  108.3 0.1 shard_map.93
  108.4 0.0 collective-permute-done.1.other_ref
  108.4 3.9 %shard_map.94 = bf16[704,1792]{1,0:T(8,128)(2,1)} custom-call(s32[1]{0:T(128)} %bitcast.4.core_ref.place_ref, bf16[704,256]{1,0:T(8,128)(2,1)} %get-tuple-element.36.score_ref, bf16[4,256,256]{2,1,0:T(8,128)(2,1)S(1)} %all_to_all.36.parts_ref.mine_ref, bf16[4,256,256]{2,1,0:T(8,128)(2,1)S(1)} %collective-permute-done.1.other_ref), custom_call_target="tpu_custom_call" | custom-call | flops 645922816 | bytes 2523136 | tf_op jit(solution)/shard_map/pallas_call | solution.py:30
  112.2 17.8 %all_to_all.41.parts_ref = bf16[16,14,256]{2,1,0:T(8,128)(2,1)S(1)} all-to-all(bf16[16,14,256]{2,1,0:T(8,128)(2,1)S(1)} %shard_map.93), channel_id=1, replica_groups=mesh['y'=4,'z'=16,'c'=2,'x'=4] {'z'}, dimensions={0} | all-to-all | bytes 229376 | tf_op jit(solution)/shard_map/all_to_all | solution.py:417
  130.1 0.6 shard_map.95
  (2 shorter events, 0.1 us)
Async XLA Ops:
  35.5 30.5 %collective-permute-start = (bf16[4,224,704]{2,1,0:T(8,128)(2,1)}, bf16[4,224,704]{2,1,0:T(8,128)(2,1)S(1)}, u32[]{:S(2)}, u32[]{:S(2)}) collective-permute-start(bf16[4,224,704]{2,1,0:T(8,128)(2,1)} %get-tuple-element.29), channel_id=1, source_target_pairs={{0,4},{4,0},{1,5},{5,1},{2,6},{6,2},{3,7},{7,3},{8,12},{12,8},{9,1... | collective-permute-start | bytes 3784712 | tf_op jit(solution)/shard_map/ppermute | solution.py:284
  66.0 24.0 %copy-start = (bf16[4,224,704]{2,1,0:T(8,128)(2,1)}, bf16[4,224,704]{2,1,0:T(8,128)(2,1)S(1)}, u32[]{:S(2)}) copy-start(bf16[4,224,704]{2,1,0:T(8,128)(2,1)S(1)} %collective-permute-done.other_ref) | copy-start | bytes 3784708
  93.2 15.2 %collective-permute-start.1 = (bf16[4,256,256]{2,1,0:T(8,128)(2,1)S(1)}, bf16[4,256,256]{2,1,0:T(8,128)(2,1)S(1)}, u32[]{:S(2)}, u32[]{:S(2)}) collective-permute-start(bf16[4,256,256]{2,1,0:T(8,128)(2,1)S(1)} %all_to_all.36.parts_ref.mine_ref), channel_id=1, source_target_pairs={{0,4},{4,0},{1,5},{5,1},{2,6},{6,2},{3,7},{7,3},{8,12},{12,8},{9,1... | collective-permute-start | bytes 1572872 | tf_op jit(solution)/shard_map/ppermute | solution.py:284

commit v5 on v4

--- a/solution.py
+++ b/solution.py
@@ -137,12 +137,6 @@
     total = total * gains_ref[0:1, :]
     for member in range(out_ref.shape[0]):
         out_ref[member] = total
-
-
-def sum_kernel(parts_ref, out_ref):
-    total = jnp.sum(parts_ref[...], axis=0)
-    for copy in range(out_ref.shape[0]):
-        out_ref[copy] = total
 
 
 def score_kernel(
@@ -349,16 +343,11 @@
     gathered, other_half = lax.optimization_barrier((gathered, other_half))
     partial_col = call(
         functools.partial(first_col_kernel, ratio=ratio, tokens=tokens),
-        kept((along, 1, experts), F32),
+        kept((along * across, 1, experts), F32),
         gathered,
         gains,
     )
-    partial_col = call(
-        sum_kernel,
-        kept((across, 1, experts), F32),
-        lax.all_to_all(partial_col, "z", 0, 0, tiled=True),
-    )
-    first_col = lax.all_to_all(partial_col, "y", 0, 0, tiled=True)
+    first_col = lax.all_to_all(partial_col, ("z", "y"), 0, 0, tiled=True)
 
     made = (across, along * rows, experts)
     score, products = call(

time: 131 us -> 128 us (0.977)
  blocking collectives: 112 us -> 108 us
    all_to_all x2 -> x1, blocking collectives: 23 us -> 20 us  [body(): first_col = lax.all_to_all(partial_col, ('z', 'y'), 0, 0, tiled=True)]
    pallas_call x10 -> x9, Pallas kernels: 14.5 us -> 14.6 us  [call(): pl.pallas_call(kernel, out_shape=shapes, cost_estimate=pl.CostEstimate(fl...]
where the time goes in v5:
time: 128 us; the launch traced here: 127 us
  blocking collectives  108 us (84%)
  Pallas kernels  14.6 us (11%)
  starting transfers between devices  3.83 us (3%)
    all_to_all x1, blocking collectives, body(): along_parts = lax.all_to_all(sent, 'z', 0, 0, tiled=True)  29.2 us
    all_to_all x1, blocking collectives, body(): first_col = lax.all_to_all(partial_col, ('z', 'y'), 0, 0, tiled=True)  20 us
    all_to_all x1, blocking collectives, body(): far = lax.all_to_all(far, 'z', 0, 0, tiled=True)  17.5 us
    pallas_call x9, Pallas kernels, call(): pl.pallas_call(kernel, out_shape=shapes, cost_estimate=pl.CostEstimate(fl...  14.6 us
    all_to_all x1, blocking collectives, body(): across_parts = lax.all_to_all(sent, 'y', 0, 0, tiled=True)  14.4 us
    all_to_all x1, blocking collectives, body(): near = lax.all_to_all(products, 'y', 0, 0, tiled=True)  13.2 us
    all_to_all x1, blocking collectives, body(): gathered = lax.all_to_all(sent, 'x', 0, 0, tiled=True)  11.7 us
    ppermute x2, starting transfers between devices, ahead(): lax.ppermute(array, axis, [(at, (at + step) % size) for at in range(size)])  3.83 us
  transfers between devices with their start and end apart: 2, of which 0 were waited for; matrix products, arithmetic and copies ran while one was open for 0% of the time, Pallas kernels for 0%

profile of v5, /device:TPU:32, one launch (start us, length us, event | category | flops | bytes accessed | tf_op | source)
XLA Modules:
  0.0 127.4 jit_solution(11508818416677739018)
XLA Ops:
  0.6 1.2 shard_map.86
  1.9 29.2 %all_to_all.30.parts_ref = bf16[16,16,256]{2,1,0:T(8,128)(2,1)S(1)} all-to-all(bf16[16,16,256]{2,1,0:T(8,128)(2,1)S(1)} %get-tuple-element.23), channel_id=1, replica_groups=mesh['y'=4,'z'=16,'c'=2,'x'=4] {'z'}, dimensions={0} | all-to-all | bytes 262144 | tf_op jit(solution)/shard_map/all_to_all | solution.py:309
  31.1 4.4 %shard_map.88 = (bf16[4,224,704]{2,1,0:T(8,128)(2,1)S(1)}, bf16[4,224,704]{2,1,0:T(8,128)(2,1)}) custom-call(s32[1]{0:T(128)} %bitcast.4.core_ref.place_ref, bf16[704,1792]{1,0:T(8,128)(2,1)} %hidden_ref), custom_call_target="tpu_custom_call" | custom-call | flops 2260729856 | bytes 5046272 | tf_op jit(solution)/shard_map/pallas_call | solution.py:30
  35.5 1.9 %collective-permute-start = (bf16[4,224,704]{2,1,0:T(8,128)(2,1)}, bf16[4,224,704]{2,1,0:T(8,128)(2,1)S(1)}, u32[]{:S(2)}, u32[]{:S(2)}) collective-permute-start(bf16[4,224,704]{2,1,0:T(8,128)(2,1)} %get-tuple-element.29), channel_id=1, source_target_pairs={{0,4},{4,0},{1,5},{5,1},{2,6},{6,2},{3,7},{7,3},{8,12},{12,8},{9,1... | collective-permute-start | bytes 3784712 | tf_op jit(solution)/shard_map/ppermute | solution.py:278
  37.4 0.1 shard_map.87
  37.5 14.4 %all_to_all.31.parts_ref.mine_ref = bf16[4,256,256]{2,1,0:T(8,128)(2,1)S(1)} all-to-all(bf16[4,256,256]{2,1,0:T(8,128)(2,1)S(1)} %shard_map.87), channel_id=1, replica_groups=mesh['y'=4,'z'=16,'c'=2,'x'=4] {'y'}, dimensions={0} | all-to-all | bytes 1048576 | tf_op jit(solution)/shard_map/all_to_all | solution.py:333
  51.9 11.7 %all_to_all.32 = bf16[4,192,256]{2,1,0:T(8,128)(2,1)S(1)} all-to-all(bf16[4,192,256]{2,1,0:T(8,128)(2,1)S(1)} %shard_map.89), channel_id=1, replica_groups=mesh['y'=4,'z'=16,'c'=2,'x'=4] {'x'}, dimensions={0} | all-to-all | bytes 786432 | tf_op jit(solution)/shard_map/all_to_all | solution.py:341
  63.6 2.4 %all_gather.3.gathered_ref = bf16[8,192,256]{2,1,0:T(8,128)(2,1)S(1)} all-gather(bf16[4,192,256]{2,1,0:T(8,128)(2,1)S(1)} %all_to_all.32), channel_id=1, replica_groups=mesh['y'=4,'z'=16,'c'=2,'x'=4] {'c'}, dimensions={0}, use_global_device_ids=true | all-gather | bytes 1179648 | tf_op jit(solution)/shard_map/all_gather | solution.py:342
  66.0 0.0 collective-permute-done.other_ref
  66.0 0.0 copy-start
  66.0 1.0 shard_map.90
  67.0 20.0 %all_to_all.33.first_col_ref = f32[64,1,256]{2,1,0:T(1,128)S(1)} all-to-all(f32[64,1,256]{2,1,0:T(1,128)S(1)} %shard_map.90), channel_id=1, replica_groups=mesh['y'=4,'z'=16,'c'=2,'x'=4] {'z','y'}, dimensions={0} | all-to-all | bytes 131072 | tf_op jit(solution)/shard_map/all_to_all | solution.py:350
  87.0 0.0 copy-done
  87.0 3.2 %shard_map.91 = (bf16[704,256]{1,0:T(8,128)(2,1)}, bf16[4,224,256]{2,1,0:T(8,128)(2,1)}) custom-call(s32[1]{0:T(128)} %bitcast.4.core_ref.place_ref, bf16[8,192,256]{2,1,0:T(8,128)(2,1)S(1)} %all_gather.3.gathered_ref, f32[2,256]{1,0:T(2,128)S(1)} %get-tuple-element.31.gains_ref, f32[64,1,256]{2,1,0:T(1,128)S(1)} %all_to_all.33.first_col_ref, ...), custom_call_target="tpu_custom_call" | custom-call | flops 645922816 | bytes 2523136 | tf_op jit(solution)/shard_map/pallas_call | solution.py:30
  90.2 1.9 %collective-permute-start.1 = (bf16[4,256,256]{2,1,0:T(8,128)(2,1)S(1)}, bf16[4,256,256]{2,1,0:T(8,128)(2,1)S(1)}, u32[]{:S(2)}, u32[]{:S(2)}) collective-permute-start(bf16[4,256,256]{2,1,0:T(8,128)(2,1)S(1)} %all_to_all.31.parts_ref.mine_ref), channel_id=1, source_target_pairs={{0,4},{4,0},{1,5},{5,1},{2,6},{6,2},{3,7},{7,3},{8,12},{12,8},{9,1... | collective-permute-start | bytes 1572872 | tf_op jit(solution)/shard_map/ppermute | solution.py:278
  92.1 13.2 %all_to_all.34.parts_ref = bf16[4,224,256]{2,1,0:T(8,128)(2,1)S(1)} all-to-all(bf16[4,224,256]{2,1,0:T(8,128)(2,1)} %get-tuple-element.34), channel_id=1, replica_groups=mesh['y'=4,'z'=16,'c'=2,'x'=4] {'y'}, dimensions={0} | all-to-all | bytes 917504 | tf_op jit(solution)/shard_map/all_to_all | solution.py:378
  105.3 0.1 shard_map.92
  105.4 0.0 collective-permute-done.1.other_ref
  105.4 3.9 %shard_map.93 = bf16[704,1792]{1,0:T(8,128)(2,1)} custom-call(s32[1]{0:T(128)} %bitcast.4.core_ref.place_ref, bf16[704,256]{1,0:T(8,128)(2,1)} %get-tuple-element.36.score_ref, bf16[4,256,256]{2,1,0:T(8,128)(2,1)S(1)} %all_to_all.31.parts_ref.mine_ref, bf16[4,256,256]{2,1,0:T(8,128)(2,1)S(1)} %collective-permute-done.1.other_ref), custom_call_target="tpu_custom_call" | custom-call | flops 645922816 | bytes 2523136 | tf_op jit(solution)/shard_map/pallas_call | solution.py:30
  109.2 17.5 %all_to_all.35.parts_ref = bf16[16,14,256]{2,1,0:T(8,128)(2,1)S(1)} all-to-all(bf16[16,14,256]{2,1,0:T(8,128)(2,1)S(1)} %shard_map.92), channel_id=1, replica_groups=mesh['y'=4,'z'=16,'c'=2,'x'=4] {'z'}, dimensions={0} | all-to-all | bytes 229376 | tf_op jit(solution)/shard_map/all_to_all | solution.py:406
  126.8 0.6 shard_map.94
  (1 shorter events, 0.0 us)
Async XLA Ops:
  35.5 30.5 %collective-permute-start = (bf16[4,224,704]{2,1,0:T(8,128)(2,1)}, bf16[4,224,704]{2,1,0:T(8,128)(2,1)S(1)}, u32[]{:S(2)}, u32[]{:S(2)}) collective-permute-start(bf16[4,224,704]{2,1,0:T(8,128)(2,1)} %get-tuple-element.29), channel_id=1, source_target_pairs={{0,4},{4,0},{1,5},{5,1},{2,6},{6,2},{3,7},{7,3},{8,12},{12,8},{9,1... | collective-permute-start | bytes 3784712 | tf_op jit(solution)/shard_map/ppermute | solution.py:278
  66.0 21.0 %copy-start = (bf16[4,224,704]{2,1,0:T(8,128)(2,1)}, bf16[4,224,704]{2,1,0:T(8,128)(2,1)S(1)}, u32[]{:S(2)}) copy-start(bf16[4,224,704]{2,1,0:T(8,128)(2,1)S(1)} %collective-permute-done.other_ref) | copy-start | bytes 3784708
  90.2 15.2 %collective-permute-start.1 = (bf16[4,256,256]{2,1,0:T(8,128)(2,1)S(1)}, bf16[4,256,256]{2,1,0:T(8,128)(2,1)S(1)}, u32[]{:S(2)}, u32[]{:S(2)}) collective-permute-start(bf16[4,256,256]{2,1,0:T(8,128)(2,1)S(1)} %all_to_all.31.parts_ref.mine_ref), channel_id=1, source_target_pairs={{0,4},{4,0},{1,5},{5,1},{2,6},{6,2},{3,7},{7,3},{8,12},{12,8},{9,1... | collective-permute-start | bytes 1572872 | tf_op jit(solution)/shard_map/ppermute | solution.py:278
